TPU v7x, 32 devices: a whole 2x2x4 slice. The times are simulated.
32 devices in a mesh: scan: 8 (over z, y), grp: 4 (over x, core).
Axes of the slice: x: 2, y: 2, z: 4, core: 2. Of those that a mesh axis runs over, the one named last changes fastest.
Arguments:
- samples: float32 [128, 64, 6, 128], P('scan', 'grp'), may hold values from -6 to 6
- point_count: int32 [128], P('scan'), may hold values from 4096 to 8192
- corr_scan: int32 [128, 64], P('scan', 'grp'), may hold values from 0 to 127, as said below
- corr_tile: int32 [128, 64], P('scan', 'grp'), may hold values from 0 to 63
- corr_src: int32 [128, 64, 128], P('scan', 'grp'), may hold values from 0 to 2047
Outputs:
- hessian: float32 [128, 6, 6, 128], P('scan', None, None, 'grp')
- gradient: float32 [128, 6], P(('scan', 'grp'))
Inputs may be any that keep to these rules, and one draw needn't show every extreme that they name: Never the scan of the entry's own row. A named tile is held by the device with scan index corr_scan // 16 and grp index corr_tile // 16; the 256 entries of one device name at most 16 tiles held by any one device, and in every draw some device is named exactly 16 times by every device.
All inputs are finite; a program needn't handle non-finite values.
Results may differ from a plain program's by a relative error of at most 0.00021.
Values sent between devices are 32-bit elements; how exact they have to be, the bound alone decides.
A program may use at most 64 MiB of HBM per device.

v0:
```python
import jax
import jax.numpy as jnp
from jax import lax
from jax.sharding import PartitionSpec as P


def pair_blocks(pos_x, pos_y, pos_z, source_mask, tile_data):
    diff_x = pos_x - tile_data[:, 0, :]
    diff_y = pos_y - tile_data[:, 1, :]
    diff_z = pos_z - tile_data[:, 2, :]
    normal_x = tile_data[:, 3, :]
    normal_y = tile_data[:, 4, :]
    normal_z = tile_data[:, 5, :]
    residual = normal_x * diff_x + normal_y * diff_y + normal_z * diff_z
    weight = source_mask / (1.0 + residual * residual)
    jacobian = jnp.stack(
        [
            pos_y * normal_z - pos_z * normal_y,
            pos_z * normal_x - pos_x * normal_z,
            pos_x * normal_y - pos_y * normal_x,
            normal_x,
            normal_y,
            normal_z,
        ],
        axis=1,
    )
    blocks = jnp.einsum(
        "nik,njk->nij", jacobian * weight[:, None, :], jacobian, precision=lax.Precision.HIGHEST
    )
    vectors = jnp.einsum("nik,nk->ni", jacobian, weight * residual, precision=lax.Precision.HIGHEST)
    return (blocks.reshape(-1, 36), vectors)


def pick_points(samples, point_ids):
    scan_local = samples.shape[0]
    tiles_local = samples.shape[1]
    group_points = tiles_local * 128
    pick_total = point_ids.shape[1]
    block = pick_total
    while block > 128 and block % 2 == 0 and (group_points * block > 4194304):
        block = block // 2
    positions = samples[:, :, 0:3, :].transpose(0, 2, 1, 3).reshape(scan_local, 3, group_points)
    point_iota = jnp.arange(group_points, dtype=jnp.int32)[:, None]

    def one_scan(operands):
        position, picks = operands
        picks = picks.reshape(pick_total // block, block)

        def one_block(wanted):
            selector = (point_iota == wanted[None, :]).astype(jnp.float32)
            return jnp.dot(
                position,
                selector,
                precision=lax.Precision.HIGHEST,
                preferred_element_type=jnp.float32,
            )

        chosen = lax.map(one_block, picks)
        return chosen.transpose(1, 0, 2).reshape(3, pick_total)

    picked = lax.map(one_scan, (positions, point_ids))
    return picked.transpose(1, 0, 2).reshape(3, -1, 128)


def masked_tiles(samples, point_count, codes, group_index):
    tiles_local = samples.shape[1]
    safe_codes = jnp.maximum(codes, 0)
    scan_local = safe_codes // tiles_local
    tile_local = safe_codes % tiles_local
    tile_table = samples.reshape(-1, 6, 128)
    picked = tile_table[safe_codes]
    limits = point_count[scan_local]
    point_ids = (group_index * tiles_local + tile_local)[..., None] * 128 + jnp.arange(128)
    valid_rows = (point_ids < limits[..., None]).astype(jnp.float32)
    return jnp.concatenate(
        [picked[..., 0:3, :], picked[..., 3:6, :] * valid_rows[..., None, :]], axis=-2
    )


def assemble(row_ids, own_scan, other_scan, blocks, vectors, row_count, column_count):
    row_hot = (row_ids[:, None] == jnp.arange(row_count)[None, :]).astype(jnp.float32)
    columns = jnp.arange(column_count)
    column_mix = (own_scan[:, None] == columns[None, :]).astype(jnp.float32) - (
        other_scan[:, None] == columns[None, :]
    ).astype(jnp.float32)
    weighted = (row_hot[:, :, None] * blocks[:, None, :]).reshape(blocks.shape[0], row_count * 36)
    hessian = jnp.einsum(
        "sk,sc->kc", weighted, column_mix, precision=lax.Precision.HIGHEST
    ).reshape(row_count, 6, 6, column_count)
    gradient = jnp.einsum("sl,sj->lj", row_hot, vectors, precision=lax.Precision.HIGHEST)
    return (hessian, gradient)


def local(samples, point_count, corr_scan, corr_tile, corr_src):
    scan_local = samples.shape[0]
    tiles_local = samples.shape[1]
    per_scan = corr_scan.shape[1]
    request_count = scan_local * per_scan
    device_count = lax.axis_size(("scan", "grp"))
    group_count = lax.axis_size("grp")
    slot_cap = 2 * request_count // device_count
    scan_index = lax.axis_index("scan")
    group_index = lax.axis_index("grp")
    scan_total = scan_local * lax.axis_size("scan")
    group_points = tiles_local * 128
    point_ids = corr_src.reshape(scan_local, per_scan * 128)
    picked = pick_points(samples, point_ids)
    coords = [picked[0], picked[1], picked[2]]
    source_mask = (
        (group_index * group_points + point_ids < point_count[:, None])
        .astype(jnp.float32)
        .reshape(request_count, 128)
    )
    target_scan = corr_scan.reshape(-1)
    target_tile = corr_tile.reshape(-1)
    destination = target_scan // scan_local * group_count + target_tile // tiles_local
    codes = target_scan % scan_local * tiles_local + target_tile % tiles_local
    onehot = (destination[:, None] == jnp.arange(device_count)[None, :]).astype(jnp.int32)
    earlier = jnp.cumsum(onehot, axis=0) - onehot
    slot_rank = jnp.sum(earlier * onehot, axis=1)
    slot_ids = destination * slot_cap + slot_rank
    source_scan = scan_index * scan_local + jnp.arange(request_count) // per_scan
    request_ids = jnp.full((device_count * slot_cap, 2), -1, jnp.int32)
    request_ids = (
        request_ids.at[slot_ids]
        .set(jnp.stack([codes, source_scan], axis=1))
        .reshape(device_count, slot_cap, 2)
    )
    requests = lax.all_to_all(request_ids, ("scan", "grp"), split_axis=0, concat_axis=0, tiled=True)
    fetched = masked_tiles(samples, point_count, requests[..., 0], group_index)
    returned = lax.all_to_all(fetched, ("scan", "grp"), split_axis=0, concat_axis=0, tiled=True)
    my_tiles = returned.reshape(-1, 6, 128)[slot_ids]
    out_blocks, out_vectors = pair_blocks(coords[0], coords[1], coords[2], source_mask, my_tiles)
    block_buf = (
        jnp.zeros((device_count * slot_cap, 36), jnp.float32)
        .at[slot_ids]
        .set(out_blocks)
        .reshape(device_count, slot_cap, 36)
    )
    vector_buf = (
        jnp.zeros((device_count * slot_cap, 6), jnp.float32)
        .at[slot_ids]
        .set(out_vectors)
        .reshape(device_count, slot_cap, 6)
    )
    in_blocks, in_vectors = (
        lax.all_to_all(block_buf, ("scan", "grp"), split_axis=0, concat_axis=0, tiled=True),
        lax.all_to_all(vector_buf, ("scan", "grp"), split_axis=0, concat_axis=0, tiled=True),
    )
    in_codes = requests[..., 0].reshape(-1)
    in_source = requests[..., 1].reshape(-1)
    in_local = jnp.maximum(in_codes, 0) // tiles_local
    row_ids = jnp.concatenate([jnp.arange(request_count) // per_scan, in_local])
    own_scan = scan_index * scan_local + row_ids
    other_scan = jnp.concatenate([target_scan, in_source])
    all_blocks = jnp.concatenate([out_blocks, in_blocks.reshape(-1, 36)], axis=0)
    all_vectors = jnp.concatenate([out_vectors, -in_vectors.reshape(-1, 6)], axis=0)
    hess_part, grad_part = assemble(
        row_ids, own_scan, other_scan, all_blocks, all_vectors, scan_local, scan_total
    )
    hessian, gradient = (
        lax.psum_scatter(hess_part, "grp", scatter_dimension=3, tiled=True),
        lax.psum_scatter(grad_part, "grp", scatter_dimension=0, tiled=True),
    )
    return (hessian, gradient)


def solution(mesh):
    placed = (
        P("scan", "grp", None, None),
        P("scan"),
        P("scan", "grp"),
        P("scan", "grp"),
        P("scan", "grp", None),
    )
    return jax.shard_map(
        local,
        mesh=mesh,
        in_specs=placed,
        out_specs=(P("scan", None, None, "grp"), P(("scan", "grp"), None)),
        check_vma=False,
    )
```

profile of v0, /device:TPU:0, one launch (start us, length us, event | category | flops | bytes accessed | tf_op | source)
XLA Modules:
  0.0 203.9 jit_solution(4460691769309137609)
XLA Ops:
  15.2 7.3 %all-to-all-start = ((s32[32,16,2]{1,2,0:T(2,128)}), s32[32,16,2]{1,2,0:T(2,128)S(1)}, u32[]{:S(2)}, u32[]{:S(2)}) async-start(s32[32,16,2]{1,2,0:T(2,128)} %copy.143), calls=%async_computation | async-start | bytes 65536 | tf_op jit(solution)/shard_map/all_to_all | solution.py:129
  25.1 4.6 %all-to-all-done = s32[32,16,2]{1,2,0:T(2,128)S(1)} async-done(((s32[32,16,2]{1,2,0:T(2,128)}), s32[32,16,2]{1,2,0:T(2,128)S(1)}, u32[]{:S(2)}, u32[]{:S(2)}) %all-to-all-start) | async-done | bytes 4128 | tf_op jit(solution)/shard_map/all_to_all | solution.py:129
  30.1 3.3 %gather_fusion.1 = s32[512]{0:T(512)S(1)} fusion(s32[16]{0:T(128)S(1)} %copy-done, s32[1024]{0:T(1024)S(1)} %pad_clamp_fusion.1), kind=kCustom, calls=%fused_computation.1 | custom fusion | bytes 6144 | tf_op jit(solution)/shard_map/gather | solution.py:72
  41.0 95.8 %while.11 = (s32[]{:T(128)}, f32[16,3,2048]{2,1,0:T(4,128)S(1)}, f32[16,3,2048]{2,1,0:T(4,128)}, s32[16,2048]{1,0:T(8,128)S(1)}, s32[]{:T(128)}) while((s32[]{:T(128)}, f32[16,3,2048]{2,1,0:T(4,128)S(1)}, f32[16,3,2048]{2,1,0:T(4,128)}, s32[16,2048]{1,0:T(8,128)S(1)}, s32[]{:T(128)}) %tuple.56), condition=%wide.region_5.6_spmd.clone, body=%wide.region_4.5_spmd.clone.sunk | while | flops 155189248 | bytes 91201 | solution.py:61
  41.0 6.0 %fusion.69 = f32[16,3,2048]{2,1,0:T(4,128)S(1)} fusion(f32[16,3,2048]{2,1,0:T(4,128)S(1)} %get-tuple-element.140, s32[]{:T(128)} %get-tuple-element.139, s32[2048]{0:T(1024)S(1)} %bitcast.199, f32[16,3,2048]{2,1,0:T(4,128)} %get-tuple-element.146), kind=kOutput, calls=%fused_computation.11.clone.1 | convolution fusion | flops 155189248 | bytes 74752 | tf_op jit(solution)/shard_map/while/body/eval_jaxpr/while/body/eval_jaxpr/dot_general | solution.py:51
  47.0 6.0 %fusion.69 = f32[16,3,2048]{2,1,0:T(4,128)S(1)} fusion(f32[16,3,2048]{2,1,0:T(4,128)S(1)} %get-tuple-element.140, s32[]{:T(128)} %get-tuple-element.139, s32[2048]{0:T(1024)S(1)} %bitcast.199, f32[16,3,2048]{2,1,0:T(4,128)} %get-tuple-element.146), kind=kOutput, calls=%fused_computation.11.clone.1 | convolution fusion | flops 155189248 | bytes 74752 | tf_op jit(solution)/shard_map/while/body/eval_jaxpr/while/body/eval_jaxpr/dot_general | solution.py:51
  53.0 6.0 %fusion.69 = f32[16,3,2048]{2,1,0:T(4,128)S(1)} fusion(f32[16,3,2048]{2,1,0:T(4,128)S(1)} %get-tuple-element.140, s32[]{:T(128)} %get-tuple-element.139, s32[2048]{0:T(1024)S(1)} %bitcast.199, f32[16,3,2048]{2,1,0:T(4,128)} %get-tuple-element.146), kind=kOutput, calls=%fused_computation.11.clone.1 | convolution fusion | flops 155189248 | bytes 74752 | tf_op jit(solution)/shard_map/while/body/eval_jaxpr/while/body/eval_jaxpr/dot_general | solution.py:51
  59.0 6.0 %fusion.69 = f32[16,3,2048]{2,1,0:T(4,128)S(1)} fusion(f32[16,3,2048]{2,1,0:T(4,128)S(1)} %get-tuple-element.140, s32[]{:T(128)} %get-tuple-element.139, s32[2048]{0:T(1024)S(1)} %bitcast.199, f32[16,3,2048]{2,1,0:T(4,128)} %get-tuple-element.146), kind=kOutput, calls=%fused_computation.11.clone.1 | convolution fusion | flops 155189248 | bytes 74752 | tf_op jit(solution)/shard_map/while/body/eval_jaxpr/while/body/eval_jaxpr/dot_general | solution.py:51
  65.0 6.0 %fusion.69 = f32[16,3,2048]{2,1,0:T(4,128)S(1)} fusion(f32[16,3,2048]{2,1,0:T(4,128)S(1)} %get-tuple-element.140, s32[]{:T(128)} %get-tuple-element.139, s32[2048]{0:T(1024)S(1)} %bitcast.199, f32[16,3,2048]{2,1,0:T(4,128)} %get-tuple-element.146), kind=kOutput, calls=%fused_computation.11.clone.1 | convolution fusion | flops 155189248 | bytes 74752 | tf_op jit(solution)/shard_map/while/body/eval_jaxpr/while/body/eval_jaxpr/dot_general | solution.py:51
  70.9 6.0 %fusion.69 = f32[16,3,2048]{2,1,0:T(4,128)S(1)} fusion(f32[16,3,2048]{2,1,0:T(4,128)S(1)} %get-tuple-element.140, s32[]{:T(128)} %get-tuple-element.139, s32[2048]{0:T(1024)S(1)} %bitcast.199, f32[16,3,2048]{2,1,0:T(4,128)} %get-tuple-element.146), kind=kOutput, calls=%fused_computation.11.clone.1 | convolution fusion | flops 155189248 | bytes 74752 | tf_op jit(solution)/shard_map/while/body/eval_jaxpr/while/body/eval_jaxpr/dot_general | solution.py:51
  76.9 6.0 %fusion.69 = f32[16,3,2048]{2,1,0:T(4,128)S(1)} fusion(f32[16,3,2048]{2,1,0:T(4,128)S(1)} %get-tuple-element.140, s32[]{:T(128)} %get-tuple-element.139, s32[2048]{0:T(1024)S(1)} %bitcast.199, f32[16,3,2048]{2,1,0:T(4,128)} %get-tuple-element.146), kind=kOutput, calls=%fused_computation.11.clone.1 | convolution fusion | flops 155189248 | bytes 74752 | tf_op jit(solution)/shard_map/while/body/eval_jaxpr/while/body/eval_jaxpr/dot_general | solution.py:51
  82.9 6.0 %fusion.69 = f32[16,3,2048]{2,1,0:T(4,128)S(1)} fusion(f32[16,3,2048]{2,1,0:T(4,128)S(1)} %get-tuple-element.140, s32[]{:T(128)} %get-tuple-element.139, s32[2048]{0:T(1024)S(1)} %bitcast.199, f32[16,3,2048]{2,1,0:T(4,128)} %get-tuple-element.146), kind=kOutput, calls=%fused_computation.11.clone.1 | convolution fusion | flops 155189248 | bytes 74752 | tf_op jit(solution)/shard_map/while/body/eval_jaxpr/while/body/eval_jaxpr/dot_general | solution.py:51
  88.9 6.0 %fusion.69 = f32[16,3,2048]{2,1,0:T(4,128)S(1)} fusion(f32[16,3,2048]{2,1,0:T(4,128)S(1)} %get-tuple-element.140, s32[]{:T(128)} %get-tuple-element.139, s32[2048]{0:T(1024)S(1)} %bitcast.199, f32[16,3,2048]{2,1,0:T(4,128)} %get-tuple-element.146), kind=kOutput, calls=%fused_computation.11.clone.1 | convolution fusion | flops 155189248 | bytes 74752 | tf_op jit(solution)/shard_map/while/body/eval_jaxpr/while/body/eval_jaxpr/dot_general | solution.py:51
  94.9 6.0 %fusion.69 = f32[16,3,2048]{2,1,0:T(4,128)S(1)} fusion(f32[16,3,2048]{2,1,0:T(4,128)S(1)} %get-tuple-element.140, s32[]{:T(128)} %get-tuple-element.139, s32[2048]{0:T(1024)S(1)} %bitcast.199, f32[16,3,2048]{2,1,0:T(4,128)} %get-tuple-element.146), kind=kOutput, calls=%fused_computation.11.clone.1 | convolution fusion | flops 155189248 | bytes 74752 | tf_op jit(solution)/shard_map/while/body/eval_jaxpr/while/body/eval_jaxpr/dot_general | solution.py:51
  100.9 6.0 %fusion.69 = f32[16,3,2048]{2,1,0:T(4,128)S(1)} fusion(f32[16,3,2048]{2,1,0:T(4,128)S(1)} %get-tuple-element.140, s32[]{:T(128)} %get-tuple-element.139, s32[2048]{0:T(1024)S(1)} %bitcast.199, f32[16,3,2048]{2,1,0:T(4,128)} %get-tuple-element.146), kind=kOutput, calls=%fused_computation.11.clone.1 | convolution fusion | flops 155189248 | bytes 74752 | tf_op jit(solution)/shard_map/while/body/eval_jaxpr/while/body/eval_jaxpr/dot_general | solution.py:51
  106.9 6.0 %fusion.69 = f32[16,3,2048]{2,1,0:T(4,128)S(1)} fusion(f32[16,3,2048]{2,1,0:T(4,128)S(1)} %get-tuple-element.140, s32[]{:T(128)} %get-tuple-element.139, s32[2048]{0:T(1024)S(1)} %bitcast.199, f32[16,3,2048]{2,1,0:T(4,128)} %get-tuple-element.146), kind=kOutput, calls=%fused_computation.11.clone.1 | convolution fusion | flops 155189248 | bytes 74752 | tf_op jit(solution)/shard_map/while/body/eval_jaxpr/while/body/eval_jaxpr/dot_general | solution.py:51
  112.8 6.0 %fusion.69 = f32[16,3,2048]{2,1,0:T(4,128)S(1)} fusion(f32[16,3,2048]{2,1,0:T(4,128)S(1)} %get-tuple-element.140, s32[]{:T(128)} %get-tuple-element.139, s32[2048]{0:T(1024)S(1)} %bitcast.199, f32[16,3,2048]{2,1,0:T(4,128)} %get-tuple-element.146), kind=kOutput, calls=%fused_computation.11.clone.1 | convolution fusion | flops 155189248 | bytes 74752 | tf_op jit(solution)/shard_map/while/body/eval_jaxpr/while/body/eval_jaxpr/dot_general | solution.py:51
  118.8 6.0 %fusion.69 = f32[16,3,2048]{2,1,0:T(4,128)S(1)} fusion(f32[16,3,2048]{2,1,0:T(4,128)S(1)} %get-tuple-element.140, s32[]{:T(128)} %get-tuple-element.139, s32[2048]{0:T(1024)S(1)} %bitcast.199, f32[16,3,2048]{2,1,0:T(4,128)} %get-tuple-element.146), kind=kOutput, calls=%fused_computation.11.clone.1 | convolution fusion | flops 155189248 | bytes 74752 | tf_op jit(solution)/shard_map/while/body/eval_jaxpr/while/body/eval_jaxpr/dot_general | solution.py:51
  124.8 6.0 %fusion.69 = f32[16,3,2048]{2,1,0:T(4,128)S(1)} fusion(f32[16,3,2048]{2,1,0:T(4,128)S(1)} %get-tuple-element.140, s32[]{:T(128)} %get-tuple-element.139, s32[2048]{0:T(1024)S(1)} %bitcast.199, f32[16,3,2048]{2,1,0:T(4,128)} %get-tuple-element.146), kind=kOutput, calls=%fused_computation.11.clone.1 | convolution fusion | flops 155189248 | bytes 74752 | tf_op jit(solution)/shard_map/while/body/eval_jaxpr/while/body/eval_jaxpr/dot_general | solution.py:51
  130.8 6.0 %fusion.69 = f32[16,3,2048]{2,1,0:T(4,128)S(1)} fusion(f32[16,3,2048]{2,1,0:T(4,128)S(1)} %get-tuple-element.140, s32[]{:T(128)} %get-tuple-element.139, s32[2048]{0:T(1024)S(1)} %bitcast.199, f32[16,3,2048]{2,1,0:T(4,128)} %get-tuple-element.146), kind=kOutput, calls=%fused_computation.11.clone.1 | convolution fusion | flops 155189248 | bytes 74752 | tf_op jit(solution)/shard_map/while/body/eval_jaxpr/while/body/eval_jaxpr/dot_general | solution.py:51
  148.4 5.7 %all-to-all-start.2 = ((f32[32,1,576]{2,1,0:T(1,128)}), f32[32,1,576]{2,1,0:T(1,128)S(1)}, u32[]{:S(2)}, u32[]{:S(2)}) async-start(f32[32,1,576]{2,1,0:T(1,128)} %reshape.580), calls=%async_computation.2 | async-start | bytes 163840 | tf_op jit(solution)/shard_map/all_to_all | solution.py:147
  155.1 6.5 %all-to-all-done.2 = f32[32,1,576]{2,1,0:T(1,128)S(1)} async-done(((f32[32,1,576]{2,1,0:T(1,128)}), f32[32,1,576]{2,1,0:T(1,128)S(1)}, u32[]{:S(2)}, u32[]{:S(2)}) %all-to-all-start.2) | async-done | bytes 73760 | tf_op jit(solution)/shard_map/all_to_all | solution.py:147
  181.0 6.9 %all-to-all-done.3 = f32[32,16,6]{1,2,0:T(8,128)S(1)} async-done(((f32[32,16,6]{1,2,0:T(8,128)}), f32[32,16,6]{1,2,0:T(8,128)S(1)}, u32[]{:S(2)}, u32[]{:S(2)}) %all-to-all-start.3) | async-done | bytes 12320 | tf_op jit(solution)/shard_map/all_to_all | solution.py:148
  188.4 5.9 %all-reduce = f32[16,6]{1,0:T(8,128)S(1)} all-reduce(f32[16,6]{1,0:T(8,128)S(1)} %fusion.40), channel_id=3, replica_groups=mesh['scan'=8,'grp'=4] {'grp'}, use_global_device_ids=true, to_apply=%region_9.10.clone | all-reduce | flops 96 | bytes 768
  (140 shorter events, 52.8 us)
Async XLA Ops:
  7.2 16.4 %copy-start.1 = (f32[16,16,6,128]{3,1,2,0:T(8,128)S(1)}, f32[16,16,6,128]{3,1,2,0:T(8,128)}, u32[]{:S(2)}) copy-start(f32[16,16,6,128]{3,1,2,0:T(8,128)} %param.7) | copy-start | bytes 2359300
  15.2 14.6 %all-to-all-start = ((s32[32,16,2]{1,2,0:T(2,128)}), s32[32,16,2]{1,2,0:T(2,128)S(1)}, u32[]{:S(2)}, u32[]{:S(2)}) async-start(s32[32,16,2]{1,2,0:T(2,128)} %copy.143), calls=%async_computation | async-start | bytes 65536 | tf_op jit(solution)/shard_map/all_to_all | solution.py:129
  23.5 1.5 copy-start.3
  23.6 6.5 %copy-start = (s32[16]{0:T(128)S(1)}, s32[16]{0:T(128)}, u32[]{:S(2)}) copy-start(s32[16]{0:T(128)} %param.8) | copy-start | bytes 196
  38.0 3.0 %copy-start.4 = (f32[16,3,2048]{2,1,0:T(4,128)S(1)}, f32[16,3,2048]{2,1,0:T(4,128)}, u32[]{:S(2)}) copy-start(f32[16,3,2048]{2,1,0:T(4,128)} %custom-call.6) | copy-start | bytes 1179652
  38.0 99.7 %all-to-all-start.1 = ((f32[32,16,6,128]{3,1,2,0:T(8,128)}), f32[32,16,6,128]{3,1,2,0:T(8,128)S(1)}, u32[]{:S(2)}, u32[]{:S(2)}) async-start(f32[32,16,6,128]{3,1,2,0:T(8,128)} %pad_maximum_fusion), calls=%async_computation.1 | async-start | bytes 3145728 | tf_op jit(solution)/shard_map/all_to_all | solution.py:131
  142.7 0.8 copy-start.2
  142.9 0.7 copy-start.5
  142.9 0.8 copy-start.7
  142.9 0.8 copy-start.9
  148.4 13.2 %all-to-all-start.2 = ((f32[32,1,576]{2,1,0:T(1,128)}), f32[32,1,576]{2,1,0:T(1,128)S(1)}, u32[]{:S(2)}, u32[]{:S(2)}) async-start(f32[32,1,576]{2,1,0:T(1,128)} %reshape.580), calls=%async_computation.2 | async-start | bytes 163840 | tf_op jit(solution)/shard_map/all_to_all | solution.py:147
  154.0 40.9 %reduce-scatter.4.cloned.1.call-start = ((), (), s32[]{:S(2)}) async-start(), calls=%async_computation.5 | async-start | bytes 409600
  170.1 1.6 copy-start.6
  170.1 1.6 copy-start.8
  170.1 1.6 copy-start.10
  171.7 8.0 %copy-start.11 = (u32[32]{0:T(128)S(1)}, u32[32]{0:T(128)}, u32[]{:S(2)}) copy-start(u32[32]{0:T(128)} %constant.142) | copy-start | bytes 388
  177.1 10.8 %all-to-all-start.3 = ((f32[32,16,6]{1,2,0:T(8,128)}), f32[32,16,6]{1,2,0:T(8,128)S(1)}, u32[]{:S(2)}, u32[]{:S(2)}) async-start(f32[32,16,6]{1,2,0:T(8,128)} %copy.172), calls=%async_computation.3 | async-start | bytes 262144 | tf_op jit(solution)/shard_map/all_to_all | solution.py:148
Sparse Core Ops, SparseCore 0:
  171.8 17.4 reduce-scatter.3
where the time goes:
time: 206 us; the launch traced here: 204 us
  matrix products  103 us (50%)
  local copies, waits for them, and re-layouts  37.9 us (18%)
  starting transfers between devices  18.8 us (9%)
  waiting for transfers between devices  18.1 us (9%)
  between operations  15.2 us (7%)
  blocking collectives  5.95 us (3%)
  other arithmetic  4.39 us (2%)
    dot_general x16, matrix products, one_block(): jnp.dot(position, selector, precision=lax.Precision.HIGHEST, preferred_el...  95.4 us
    unnamed x36, local copies, waits for them, and re-layouts  8.17 us
    all_to_all x1, starting transfers between devices, local(): lax.all_to_all(request_ids, ('scan', 'grp'), split_axis=0, concat_axis=0,...  7.33 us
    all_to_all x1, waiting for transfers between devices, local(): lax.all_to_all(vector_buf, ('scan', 'grp'), split_axis=0, concat_axis=0,...  6.94 us
    all_to_all x1, waiting for transfers between devices, local(): lax.all_to_all(block_buf, ('scan', 'grp'), split_axis=0, concat_axis=0, t...  6.55 us
    unnamed x1, blocking collectives  5.95 us
    all_to_all x1, starting transfers between devices, local(): lax.all_to_all(block_buf, ('scan', 'grp'), split_axis=0, concat_axis=0, t...  5.66 us
    all_to_all x1, waiting for transfers between devices, local(): lax.all_to_all(request_ids, ('scan', 'grp'), split_axis=0, concat_axis=0,...  4.63 us
  transfers between devices with their start and end apart: 5, of which 3 were waited for; matrix products, arithmetic and copies ran while one was open for 52% of the time, Pallas kernels for 0%

commit v1 on v0

v1 whole, which is shorter than its diff:
```python
import functools

import jax
import jax.numpy as jnp
from jax import lax
from jax.experimental import pallas as pl
from jax.experimental.pallas import tpu as pltpu
from jax.sharding import PartitionSpec as P

LANES = 128
VALUES = 32
PAIRS = [(i, j) for i in range(6) for j in range(i, 6)]
VMEM = pl.BlockSpec(memory_space=pltpu.VMEM)
SMEM = pl.BlockSpec(memory_space=pltpu.SMEM)


def lane_take(table, index):
    return jnp.take_along_axis(table, index, axis=1, mode="promise_in_bounds")


def pack_kernel(cap, n_grp, samples, count, corr_scan, corr_tile, corr_src, data, meta, used):
    scan_local, tiles_local = samples.shape[0], samples.shape[1]
    per_scan = corr_src.shape[1]
    devices = meta.shape[0]
    scan_index, group_index = lax.axis_index("scan"), lax.axis_index("grp")
    first_point = group_index * tiles_local * LANES

    def clear(d, _):
        used[d] = 0
        for j in range(cap):
            meta[d, 0, j] = -1
            meta[d, 0, cap + j] = -1
        data[pl.ds(pl.multiple_of(d * cap * 4, 8), cap * 4), :] = jnp.zeros((cap * 4, LANES), jnp.float32)
        return 0

    lax.fori_loop(0, devices, clear, 0)

    def one_scan(s, _):
        wanted = corr_src[s]
        tile, lane = wanted >> 7, wanted & (LANES - 1)
        picked = [jnp.zeros((per_scan, LANES), jnp.float32)] * 3
        for t in range(tiles_local):
            hit = tile == t
            for c in range(3):
                row = jnp.broadcast_to(samples[s, t, pl.ds(c, 1), :], (per_scan, LANES))
                picked[c] = jnp.where(hit, lane_take(row, lane), picked[c])
        mask = jnp.where(first_point + wanted < count[s], 1.0, 0.0).astype(jnp.float32)
        picked.append(mask)
        for k in range(per_scan):
            b, t = corr_scan[s, k], corr_tile[s, k]
            d = b // scan_local * n_grp + t // tiles_local
            j = used[d]
            used[d] = j + 1
            meta[d, 0, j] = b % scan_local * tiles_local + t % tiles_local
            meta[d, 0, cap + j] = scan_index * scan_local + s
            base = (d * cap + j) * 4
            for c in range(4):
                data[pl.ds(base + c, 1), :] = picked[c][k : k + 1, :]
        return 0

    lax.fori_loop(0, scan_local, one_scan, 0)


def meet_all(n_grp, devices, me):
    barrier = pltpu.get_barrier_semaphore()

    def hello(k, _):
        peer = lax.rem(me + k, devices)
        pl.semaphore_signal(
            barrier, inc=1, device_id=(peer // n_grp, peer % n_grp), device_id_type=pl.DeviceIdType.MESH
        )
        return 0

    lax.fori_loop(1, devices, hello, 0)
    pl.semaphore_wait(barrier, devices - 1)


def remote(src, dst, send, recv, peer, n_grp):
    return pltpu.make_async_remote_copy(
        src_ref=src, dst_ref=dst, send_sem=send, recv_sem=recv,
        device_id=(peer // n_grp, peer % n_grp), device_id_type=pl.DeviceIdType.MESH,
    )


def swap_kernel(n_grp, rows, data, meta, data_in, meta_in, send_a, recv_a, send_b, recv_b, own):
    devices = meta.shape[0]
    me = lax.axis_index("scan") * n_grp + lax.axis_index("grp")

    def part(d):
        return pl.ds(pl.multiple_of(d * rows, rows), rows)

    meet_all(n_grp, devices, me)

    def start(k, _):
        peer = lax.rem(me + k, devices)
        remote(meta.at[peer], meta_in.at[me], send_b.at[peer], recv_b.at[me], peer, n_grp).start()
        remote(data.at[part(peer)], data_in.at[part(me)], send_a.at[peer], recv_a.at[me], peer, n_grp).start()
        return 0

    lax.fori_loop(1, devices, start, 0)
    local_a = pltpu.make_async_copy(data.at[part(me)], data_in.at[part(me)], own.at[0])
    local_b = pltpu.make_async_copy(meta.at[me], meta_in.at[me], own.at[1])
    local_a.start()
    local_b.start()
    local_a.wait()
    local_b.wait()

    def finish(k, _):
        peer = lax.rem(me + k, devices)
        a = remote(data.at[part(peer)], data_in.at[part(peer)], send_a.at[peer], recv_a.at[peer], peer, n_grp)
        b = remote(meta.at[peer], meta_in.at[peer], send_b.at[peer], recv_b.at[peer], peer, n_grp)
        a.wait_send()
        b.wait_send()
        a.wait_recv()
        b.wait_recv()
        return 0

    lax.fori_loop(1, devices, finish, 0)


def regroup(parts, width):
    groups = len(parts)
    lane = lax.broadcasted_iota(jnp.int32, parts[0].shape, 1) // width
    out = []
    for b in range(groups):
        total = parts[b]
        for g in range(groups):
            if g != b:
                total = jnp.where(lane == g, pltpu.roll(parts[g], (g - b) * width % LANES, 1), total)
        out.append(total)
    return out


def block_kernel(cap, n_grp, samples, count, meta, data, packed, tile_rows, scan_rows, sums):
    scan_local, tiles_local = samples.shape[0], samples.shape[1]
    n_scan, packed_rows = packed.shape[0], packed.shape[1]
    slots = n_scan * n_grp * cap
    width = n_grp * cap
    groups = LANES // width
    batch = 16
    scan_index, group_index = lax.axis_index("scan"), lax.axis_index("grp")
    lane = lax.broadcasted_iota(jnp.int32, (batch, LANES), 1)

    def one_batch(i, first):
        for j in range(batch):
            slot = first + i * batch + j
            d, place = slot // cap, slot % cap
            code = meta[d, 0, place]
            source = meta[d, 0, cap + place]
            safe = jnp.maximum(code, 0)
            b, t = safe // tiles_local, safe % tiles_local
            limit = count[b] - (group_index * tiles_local + t) * LANES
            partner = jnp.where(code < 0, -1, scan_index * scan_local + b)
            tile_rows[j * 8 : j * 8 + 6, :] = samples[b, t]
            tile_rows[j * 8 + 6 : j * 8 + 7, :] = jnp.full((1, LANES), limit.astype(jnp.float32))
            tile_rows[j * 8 + 7 : j * 8 + 8, :] = jnp.full((1, LANES), partner.astype(jnp.float32))
            scan_rows[j : j + 1, :] = jnp.full((1, LANES), source.astype(jnp.float32))
        rows = [tile_rows[pl.ds(c, batch, stride=8), :] for c in range(8)]
        base = (first + i * batch) * 4
        px, py, pz, mask = [data[pl.ds(base + c, batch, stride=4), :] for c in range(4)]
        valid = lane < rows[6].astype(jnp.int32)
        nx, ny, nz = [jnp.where(valid, rows[c], 0.0) for c in (3, 4, 5)]
        residual = nx * (px - rows[0]) + ny * (py - rows[1]) + nz * (pz - rows[2])
        weight = mask / (1.0 + residual * residual)
        jac = [py * nz - pz * ny, pz * nx - px * nz, px * ny - py * nx, nx, ny, nz]
        scaled = [weight * x for x in jac]
        products = [scaled[a] * jac[b] for a, b in PAIRS] + [x * residual for x in scaled]
        total = jnp.zeros((batch, LANES), jnp.float32)
        for q, product in enumerate(products):
            total = jnp.where(lane == q, jnp.sum(product, axis=1, keepdims=True), total)
        total = jnp.where(lane == 27, scan_rows[...], total)
        total = jnp.where(lane == 28, rows[7], total)
        sums[pl.ds(pl.multiple_of(i * batch, batch), batch), :] = total
        return first

    for c in range(slots // LANES):
        lax.fori_loop(0, LANES // batch, one_batch, c * LANES)
        turned = sums[...].T
        parts = [turned[g * packed_rows : (g + 1) * packed_rows, :] for g in range(groups)]
        for g, part in enumerate(regroup(parts, width)):
            packed[c * groups + g] = part


def share_kernel(n_grp, packed, by_source, by_partner, send_a, recv_a, send_b, recv_b, own):
    devices = by_source.shape[0]
    scan_index, group_index = lax.axis_index("scan"), lax.axis_index("grp")
    me = scan_index * n_grp + group_index
    meet_all(n_grp, devices, me)

    def whole(g):
        peer = scan_index * n_grp + g
        return remote(packed, by_partner.at[g], send_b.at[g], recv_b.at[g], peer, n_grp)

    for k in range(1, n_grp):
        g = lax.rem(group_index + k, n_grp)
        remote(
            packed, by_partner.at[group_index], send_b.at[g], recv_b.at[group_index], scan_index * n_grp + g, n_grp
        ).start()

    def start(k, _):
        peer = lax.rem(me + k, devices)
        remote(packed.at[peer // n_grp], by_source.at[me], send_a.at[peer], recv_a.at[me], peer, n_grp).start()
        return 0

    lax.fori_loop(1, devices, start, 0)
    local_a = pltpu.make_async_copy(packed.at[scan_index], by_source.at[me], own.at[0])
    local_b = pltpu.make_async_copy(packed, by_partner.at[group_index], own.at[1])
    local_a.start()
    local_b.start()
    local_a.wait()
    local_b.wait()

    def finish(k, _):
        peer = lax.rem(me + k, devices)
        a = remote(packed.at[peer // n_grp], by_source.at[peer], send_a.at[peer], recv_a.at[peer], peer, n_grp)
        a.wait_send()
        a.wait_recv()
        return 0

    lax.fori_loop(1, devices, finish, 0)
    for k in range(1, n_grp):
        b = whole(lax.rem(group_index + k, n_grp))
        b.wait_send()
        b.wait_recv()


def assemble_kernel(n_grp, width, by_source, by_partner, hessian, gradient, total):
    rows, columns = hessian.shape[0], hessian.shape[3]
    grad_rows = gradient.shape[0]
    packed_rows = by_source.shape[1]
    groups = LANES // width
    scan_index, group_index = lax.axis_index("scan"), lax.axis_index("grp")
    cells = rows * columns
    total[...] = jnp.zeros_like(total)
    step = 2 * groups

    def place(ids, first, size):
        local = ids - first
        return local, (local >= 0) & (local < size)

    def add(read, sign):
        def body(i, _):
            turned = []
            for half in range(2):
                parts = [read(i * step + half * groups + g) for g in range(groups)]
                turned.append(jnp.concatenate(regroup(parts, width), axis=0))
            values = jnp.concatenate(turned, axis=1)
            source, partner = values[27:28, :].astype(jnp.int32), values[28:29, :].astype(jnp.int32)
            own, other = (source, partner) if sign > 0 else (partner, source)
            row, row_ok = place(own, scan_index * rows, rows)
            plus, plus_ok = place(own, group_index * columns, columns)
            minus, minus_ok = place(other, group_index * columns, columns)
            plus = jnp.where(row_ok & plus_ok, row * columns + plus, -1)
            minus = jnp.where(row_ok & minus_ok, row * columns + minus, -1)
            grad, grad_ok = place(row, group_index * grad_rows, grad_rows)
            grad = jnp.where(row_ok & grad_ok, grad, -1)
            cell = lax.broadcasted_iota(jnp.int32, (cells, 2 * LANES), 0)
            chosen = jnp.where(cell == plus, 1.0, jnp.where(cell == minus, -1.0, 0.0))
            short = lax.broadcasted_iota(jnp.int32, (16, 2 * LANES), 0)
            chosen_grad = jnp.where(short == grad, float(sign), 0.0)
            matrix = jnp.concatenate([chosen, chosen_grad], axis=0).astype(jnp.bfloat16)
            high = values.astype(jnp.bfloat16)
            low = (values - high.astype(jnp.float32)).astype(jnp.bfloat16)
            both = jnp.concatenate([high, low], axis=0)
            total[...] += lax.dot_general(
                matrix, both, (((1,), (1,)), ((), ())), preferred_element_type=jnp.float32
            )
            return 0

        return body

    blocks = by_source.shape[0]
    n_scan = by_partner.shape[1]
    lax.fori_loop(0, blocks // step, add(lambda k: by_source[k], 1), 0)
    lax.fori_loop(0, blocks // step, add(lambda k: by_partner[k // n_scan, k % n_scan], -1), 0)
    result = total[:, 0:VALUES] + total[:, VALUES : 2 * VALUES]
    turned = result[0:cells, :].T
    where = {pair: q for q, pair in enumerate(PAIRS)}
    for i in range(6):
        ids = [where[min(i, j), max(i, j)] for j in range(6)]
        band = jnp.concatenate([turned[q : q + 1, :] for q in ids], axis=0)
        for r in range(rows):
            hessian[r, i] = band[:, r * columns : (r + 1) * columns]
    gradient[...] = result[cells : cells + grad_rows, 21:27]


def local(samples, point_count, corr_scan, corr_tile, corr_src):
    f32, i32 = jnp.float32, jnp.int32
    scan_local = samples.shape[0]
    request_count = scan_local * corr_scan.shape[1]
    n_scan, n_grp = lax.axis_size("scan"), lax.axis_size("grp")
    devices = n_scan * n_grp
    cap = 2 * request_count // devices
    width = n_grp * cap
    packed_rows = VALUES * width // LANES
    columns = scan_local * n_scan // n_grp
    grad_rows = scan_local // n_grp
    shape = jax.ShapeDtypeStruct
    dma = pltpu.SemaphoreType.DMA

    data, meta = pl.pallas_call(
        functools.partial(pack_kernel, cap, n_grp),
        out_shape=(shape((devices * cap * 4, LANES), f32), shape((devices, 1, LANES), i32)),
        in_specs=[VMEM, SMEM, SMEM, SMEM, VMEM],
        out_specs=(VMEM, SMEM),
        scratch_shapes=[pltpu.SMEM((devices,), i32)],
    )(samples, point_count, corr_scan, corr_tile, corr_src)

    data, meta = pl.pallas_call(
        functools.partial(swap_kernel, n_grp, cap * 4),
        out_shape=(shape(data.shape, f32), shape(meta.shape, i32)),
        in_specs=[VMEM, VMEM],
        out_specs=(VMEM, VMEM),
        scratch_shapes=[dma((devices,))] * 4 + [dma((2,))],
        compiler_params=pltpu.CompilerParams(collective_id=0, has_side_effects=True),
    )(data, meta)

    packed = pl.pallas_call(
        functools.partial(block_kernel, cap, n_grp),
        out_shape=shape((n_scan, packed_rows, LANES), f32),
        in_specs=[VMEM, SMEM, SMEM, VMEM],
        out_specs=VMEM,
        scratch_shapes=[
            pltpu.VMEM((LANES, LANES), f32),
            pltpu.VMEM((16, LANES), f32),
            pltpu.VMEM((LANES, LANES), f32),
        ],
    )(samples, point_count, meta, data)

    by_source, by_partner = pl.pallas_call(
        functools.partial(share_kernel, n_grp),
        out_shape=(
            shape((devices, packed_rows, LANES), f32),
            shape((n_grp, n_scan, packed_rows, LANES), f32),
        ),
        in_specs=[VMEM],
        out_specs=(VMEM, VMEM),
        scratch_shapes=[dma((devices,))] * 2 + [dma((n_grp,))] * 2 + [dma((2,))],
        compiler_params=pltpu.CompilerParams(collective_id=1, has_side_effects=True),
    )(packed)

    return pl.pallas_call(
        functools.partial(assemble_kernel, n_grp, width),
        out_shape=(shape((scan_local, 6, 6, columns), f32), shape((grad_rows, 6), f32)),
        in_specs=[VMEM, VMEM],
        out_specs=(VMEM, VMEM),
        scratch_shapes=[pltpu.VMEM((scan_local * columns + 16, 2 * VALUES), f32)],
    )(by_source, by_partner)


def solution(mesh):
    placed = (
        P("scan", "grp", None, None),
        P("scan"),
        P("scan", "grp"),
        P("scan", "grp"),
        P("scan", "grp", None),
    )
    return jax.shard_map(
        local,
        mesh=mesh,
        in_specs=placed,
        out_specs=(P("scan", None, None, "grp"), P(("scan", "grp"), None)),
        check_vma=False,
    )
```

time: 206 us -> 83.6 us (0.41)
  matrix products: 103 us -> 0 us
  Pallas kernels: 0 us -> 78.4 us
  local copies, waits for them, and re-layouts: 37.9 us -> 4.17 us
  starting transfers between devices: 18.8 us -> 0 us
  waiting for transfers between devices: 18.1 us -> 0 us
  between operations: 15.2 us -> 0.65 us
  blocking collectives: 5.95 us -> 0 us
  other arithmetic: 4.39 us -> 0 us
    dot_general x20 -> x0, matrix products: 103 us -> none  [the longest x16 95.4 us: one_block(): jnp.dot(position, selector, precision=lax.Precision.HIGHEST, preferred_el...]
    pallas_call x0 -> x5, Pallas kernels: none -> 78.4 us  [the longest x1 28.1 us: local(): pl.pallas_call(functools.partial(swap_kernel, n_grp, cap * 4), out_shape=...]
    all_to_all x4 -> x0, starting transfers between devices: 18.6 us -> none  [the longest x1 7.33 us: local(): lax.all_to_all(request_ids, ('scan', 'grp'), split_axis=0, concat_axis=0,...]
    all_to_all x4 -> x0, waiting for transfers between devices: 18.1 us -> none  [the longest x1 6.94 us: local(): lax.all_to_all(vector_buf, ('scan', 'grp'), split_axis=0, concat_axis=0,...]
    reshape x13 -> x0, local copies, waits for them, and re-layouts: 8.18 us -> none  [the longest x3 2.41 us: local(): target_scan = corr_scan.reshape(-1)]
    gather x4 -> x0, local copies, waits for them, and re-layouts: 7.65 us -> none  [the longest x2 3.43 us: masked_tiles(): limits = point_count[scan_local]]
    unnamed x1 -> x0, blocking collectives: 5.95 us -> none
    unnamed x36 -> x1, local copies, waits for them, and re-layouts: 8.17 us -> 2.36 us
  transfers between devices with their start and end apart: 5 -> 0, of which waited for: 3 -> 0; matrix products, arithmetic and copies ran while one was open for 52% -> 0% of each run, Pallas kernels for 0% -> 0%
where the time goes in v1:
time: 83.6 us; the launch traced here: 83.2 us
  Pallas kernels  78.4 us (94%)
  local copies, waits for them, and re-layouts  4.17 us (5%)
    pallas_call x1, Pallas kernels, local(): pl.pallas_call(functools.partial(swap_kernel, n_grp, cap * 4), out_shape=...  28.1 us
    pallas_call x1, Pallas kernels, local(): pl.pallas_call(functools.partial(share_kernel, n_grp), out_shape=(shape((...  20.8 us
    pallas_call x1, Pallas kernels, local(): pl.pallas_call(functools.partial(block_kernel, cap, n_grp), out_shape=sha...  14.2 us
    pallas_call x1, Pallas kernels, local(): pl.pallas_call(functools.partial(pack_kernel, cap, n_grp), out_shape=(sha...  8.06 us
    pallas_call x1, Pallas kernels, local(): pl.pallas_call(functools.partial(assemble_kernel, n_grp, width), out_shap...  7.35 us
    unnamed x1, local copies, waits for them, and re-layouts  2.36 us
    pallas_call x1, local copies, waits for them, and re-layouts, local(): pl.pallas_call(functools.partial(assemble_kernel, n_grp, width), out_shap...  1.81 us

profile of v1, /device:TPU:0, one launch (start us, length us, event | category | flops | bytes accessed | tf_op | source)
XLA Modules:
  0.0 83.2 jit_solution(14658386392288279035)
XLA Ops:
  0.6 2.4 %copy.8.samples = f32[16,16,6,128]{3,2,1,0:T(8,128)} copy(f32[16,16,6,128]{3,1,2,0:T(8,128)} %param.5) | data formatting | bytes 1572864 | tf_op args[0]
  3.0 8.1 %shard_map.68 = (f32[2048,128]{1,0:T(8,128)}, s32[32,1,128]{2,1,0:T(1,128)}) custom-call(f32[16,16,6,128]{3,2,1,0:T(8,128)} %copy.8.samples, s32[16]{0:T(128)} %count.3, s32[16,16]{1,0:T(8,128)} %corr_scan.1, s32[16,16]{1,0:T(8,128)} %corr_tile.1, s32[16,16,128]{2,1,0:T(8,128)} %corr_src.1), custom_call_target="tpu_custom_call" | custom-call | tf_op jit(solution)/shard_map/pallas_call | solution.py:301
  11.1 28.1 %shard_map.69 = (f32[2048,128]{1,0:T(8,128)}, s32[32,1,128]{2,1,0:T(1,128)}) custom-call(f32[2048,128]{1,0:T(8,128)} %get-tuple-element.8.data, s32[32,1,128]{2,1,0:T(1,128)} %get-tuple-element.9.meta), custom_call_target="tpu_custom_call" | custom-call | tf_op jit(solution)/shard_map/pallas_call | solution.py:309
  39.1 14.2 %shard_map.70.packed = f32[8,16,128]{2,1,0:T(8,128)} custom-call(f32[16,16,6,128]{3,2,1,0:T(8,128)} %copy.8.samples, s32[16]{0:T(128)} %count.3, s32[32,1,128]{2,1,0:T(1,128)} %get-tuple-element.10.meta, f32[2048,128]{1,0:T(8,128)} %get-tuple-element.11.data), custom_call_target="tpu_custom_call" | custom-call | tf_op jit(solution)/shard_map/pallas_call | solution.py:318
  53.3 20.8 %shard_map.71 = (f32[32,16,128]{2,1,0:T(8,128)}, f32[4,8,16,128]{3,2,1,0:T(8,128)}) custom-call(f32[8,16,128]{2,1,0:T(8,128)} %shard_map.70.packed), custom_call_target="tpu_custom_call" | custom-call | tf_op jit(solution)/shard_map/pallas_call | solution.py:330
  74.1 7.4 %shard_map.72 = (f32[16,6,6,32]{3,2,1,0:T(8,128)}, f32[4,6]{1,0:T(4,128)}) custom-call(f32[32,16,128]{2,1,0:T(8,128)} %get-tuple-element.12.by_source, f32[4,8,16,128]{3,2,1,0:T(8,128)} %get-tuple-element.13.by_partner), custom_call_target="tpu_custom_call" | custom-call | tf_op jit(solution)/shard_map/pallas_call | solution.py:342
  81.4 1.8 %copy.9 = f32[16,6,6,32]{3,0,2,1:T(8,128)} copy(f32[16,6,6,32]{3,2,1,0:T(8,128)} %get-tuple-element.14) | data formatting | bytes 147456 | tf_op jit(solution)/shard_map/pallas_call | solution.py:342

commit v2 on v1

v2 whole, which is shorter than its diff:
```python
import functools

import jax
import jax.numpy as jnp
from jax import lax
from jax.experimental import pallas as pl
from jax.experimental.pallas import tpu as pltpu
from jax.sharding import PartitionSpec as P

LANES = 128
VALUES = 32
PAIRS = [(i, j) for i in range(6) for j in range(i, 6)]
VMEM = pl.BlockSpec(memory_space=pltpu.VMEM)
SMEM = pl.BlockSpec(memory_space=pltpu.SMEM)


def halves(value, size):
    if size & (size - 1):
        return value // size, value % size
    return value >> (size.bit_length() - 1), value & (size - 1)


def lane_take(table, index):
    return jnp.take_along_axis(table, index, axis=1, mode="promise_in_bounds")


def pack_kernel(cap, n_grp, samples, count, corr_scan, corr_tile, corr_src, data, meta, used):
    scan_local, tiles_local = samples.shape[0], samples.shape[2]
    per_scan = corr_src.shape[1]
    devices = meta.shape[0]
    scan_index, group_index = lax.axis_index("scan"), lax.axis_index("grp")
    first_point = group_index * tiles_local * LANES

    def clear(d, _):
        used[d] = 0
        for j in range(cap):
            meta[d, 0, j] = -1
            meta[d, 0, cap + j] = 0
            meta[d, 0, 2 * cap + j] = -1
        data[pl.ds(pl.multiple_of(d * cap * 4, 8), cap * 4), :] = jnp.zeros((cap * 4, LANES), jnp.float32)
        return 0

    lax.fori_loop(0, devices, clear, 0)

    def one_scan(s, _):
        wanted = corr_src[s]
        tile, lane = wanted >> 7, wanted & (LANES - 1)
        picked = [jnp.zeros((per_scan, LANES), jnp.float32)] * 3
        for t in range(tiles_local):
            hit = tile == t
            for c in range(3):
                row = jnp.broadcast_to(samples[s, c, pl.ds(t, 1), :], (per_scan, LANES))
                picked[c] = jnp.where(hit, lane_take(row, lane), picked[c])
        mask = jnp.where(first_point + wanted < count[s], 1.0, 0.0).astype(jnp.float32)
        picked.append(mask)
        for k in range(per_scan):
            b, t = corr_scan[s, k], corr_tile[s, k]
            (b_dev, b_loc), (t_dev, t_loc) = halves(b, scan_local), halves(t, tiles_local)
            d = b_dev * n_grp + t_dev
            j = used[d]
            used[d] = j + 1
            meta[d, 0, j] = b_loc
            meta[d, 0, cap + j] = t_loc
            meta[d, 0, 2 * cap + j] = scan_index * scan_local + s
            base = (d * cap + j) * 4
            for c in range(4):
                data[pl.ds(base + c, 1), :] = picked[c][k : k + 1, :]
        return 0

    lax.fori_loop(0, scan_local, one_scan, 0)


def meet_all(n_grp, devices, me):
    barrier = pltpu.get_barrier_semaphore()

    def hello(k, _):
        peer = lax.rem(me + k, devices)
        pl.semaphore_signal(
            barrier, inc=1, device_id=(peer // n_grp, peer % n_grp), device_id_type=pl.DeviceIdType.MESH
        )
        return 0

    lax.fori_loop(1, devices, hello, 0)
    pl.semaphore_wait(barrier, devices - 1)


def remote(src, dst, send, recv, peer, n_grp):
    return pltpu.make_async_remote_copy(
        src_ref=src, dst_ref=dst, send_sem=send, recv_sem=recv,
        device_id=(peer // n_grp, peer % n_grp), device_id_type=pl.DeviceIdType.MESH,
    )


def exchange_kernel(
    cap, n_grp, samples, count, data, meta, by_source, by_partner,
    data_in, meta_in, codes, comps, sums, packed,
    send_data, recv_data, send_meta, recv_meta, send_src, recv_src, send_part, recv_part, own,
):
    scan_local, tiles_local = samples.shape[0], samples.shape[2]
    n_scan, packed_rows = packed.shape[0], packed.shape[1]
    devices = n_scan * n_grp
    rows = cap * 4
    width = n_grp * cap
    groups = LANES // width
    batch = 16
    scan_index, group_index = lax.axis_index("scan"), lax.axis_index("grp")
    me = scan_index * n_grp + group_index
    lane = lax.broadcasted_iota(jnp.int32, (batch, LANES), 1)
    packed_lane = lax.broadcasted_iota(jnp.int32, (packed_rows, LANES), 1) // width

    def part(d):
        return pl.ds(pl.multiple_of(d * rows, rows), rows)

    def send_one(src, dst_index, send_index, recv_index, peer):
        return remote(
            data.at[part(src)], data_in.at[part(dst_index)], send_data.at[send_index], recv_data.at[recv_index], peer, n_grp
        )

    def send_code(src, dst_index, send_index, recv_index, peer):
        return remote(
            meta.at[src], meta_in.at[dst_index], send_meta.at[send_index], recv_meta.at[recv_index], peer, n_grp
        )

    def to_source(row, holder, peer, recv_index):
        return remote(packed.at[row], by_source.at[holder], send_src.at[peer], recv_src.at[recv_index], peer, n_grp)

    def to_partner(row, at, g):
        peer = scan_index * n_grp + g
        return remote(
            packed.at[row], by_partner.at[at, row], send_part.at[g, row], recv_part.at[at, row], peer, n_grp
        )

    meet_all(n_grp, devices, me)

    def start_meta(k, _):
        peer = lax.rem(me + k, devices)
        send_code(peer, me, peer, me, peer).start()
        return 0

    def start_data(k, _):
        peer = lax.rem(me + k, devices)
        send_one(peer, me, peer, me, peer).start()
        return 0

    def wait_meta(k, _):
        peer = lax.rem(me + k, devices)
        copy = send_code(peer, peer, peer, peer, peer)
        copy.wait_send()
        copy.wait_recv()
        return 0

    lax.fori_loop(1, devices, start_meta, 0)
    lax.fori_loop(1, devices, start_data, 0)
    own_data = pltpu.make_async_copy(data.at[part(me)], data_in.at[part(me)], own.at[0])
    own_meta = pltpu.make_async_copy(meta.at[me], meta_in.at[me], own.at[1])
    own_data.start()
    own_meta.start()
    sums[...] = jnp.zeros_like(sums)
    own_data.wait()
    own_meta.wait()
    lax.fori_loop(1, devices, wait_meta, 0)
    to_scalar = pltpu.make_async_copy(meta_in, codes, own.at[2])
    to_scalar.start()
    to_scalar.wait()

    def one_batch(i, row):
        for j in range(batch):
            step, place = halves(i * batch + j, cap)
            d = row * n_grp + step
            b, t = codes[d, 0, place], codes[d, 0, cap + place]
            source = codes[d, 0, 2 * cap + place]
            safe = jnp.maximum(b, 0)
            limit = count[safe] - (group_index * tiles_local + t) * LANES
            partner = jnp.where(b < 0, -1, scan_index * scan_local + b)
            for c in range(6):
                comps[c, j : j + 1, :] = samples[safe, c, pl.ds(t, 1), :]
            comps[6, j : j + 1, :] = jnp.full((1, LANES), limit.astype(jnp.float32))
            comps[7, j : j + 1, :] = jnp.full((1, LANES), partner.astype(jnp.float32))
            comps[8, j : j + 1, :] = jnp.full((1, LANES), source.astype(jnp.float32))
        base = (row * width + i * batch) * 4
        px, py, pz, mask = [data_in[pl.ds(base + c, batch, stride=4), :] for c in range(4)]
        valid = lane < comps[6].astype(jnp.int32)
        nx, ny, nz = [jnp.where(valid, comps[c], 0.0) for c in (3, 4, 5)]
        residual = nx * (px - comps[0]) + ny * (py - comps[1]) + nz * (pz - comps[2])
        weight = mask / (1.0 + residual * residual)
        jac = [py * nz - pz * ny, pz * nx - px * nz, px * ny - py * nx, nx, ny, nz]
        scaled = [weight * x for x in jac]
        products = [scaled[a] * jac[b] for a, b in PAIRS] + [x * residual for x in scaled]
        total = jnp.zeros((batch, LANES), jnp.float32)
        for q, product in enumerate(products):
            total = jnp.where(lane == q, jnp.sum(product, axis=1, keepdims=True), total)
        total = jnp.where(lane == 27, comps[8], total)
        total = jnp.where(lane == 28, comps[7], total)
        sums[pl.ds(pl.multiple_of(i * batch, batch), batch), :] = total
        return row

    def one_row(k, _):
        row = lax.rem(scan_index + n_scan - k, n_scan)
        for g in range(n_grp):
            source = row * n_grp + g

            @pl.when(source != me)
            def _():
                send_one(source, source, source, source, source).wait_recv()

        lax.fori_loop(0, width // batch, one_batch, row)
        turned = sums[...].T
        result = turned[0:packed_rows, :]
        for g in range(1, groups):
            moved = pltpu.roll(turned[g * packed_rows : (g + 1) * packed_rows, :], g * width, 1)
            result = jnp.where(packed_lane == g, moved, result)
        packed[row] = result
        by_partner[group_index, row] = result
        for g in range(n_grp):
            peer = row * n_grp + g

            @pl.when(peer != me)
            def _():
                to_source(row, me, peer, me).start()

        @pl.when(row == scan_index)
        def _():
            by_source[me] = result

        for g in range(1, n_grp):
            to_partner(row, group_index, lax.rem(group_index + g, n_grp)).start()
        return 0

    lax.fori_loop(0, n_scan, one_row, 0)

    def finish(k, _):
        peer = lax.rem(me + k, devices)
        send_one(peer, peer, peer, peer, peer).wait_send()
        copy = to_source(0, peer, peer, peer)
        copy.wait_send()
        copy.wait_recv()
        return 0

    lax.fori_loop(1, devices, finish, 0)

    def finish_partner(row, _):
        for k in range(1, n_grp):
            g = lax.rem(group_index + k, n_grp)
            copy = to_partner(row, g, g)
            copy.wait_send()
            copy.wait_recv()
        return 0

    lax.fori_loop(0, n_scan, finish_partner, 0)


def regroup(parts, width):
    groups = len(parts)
    lane = lax.broadcasted_iota(jnp.int32, parts[0].shape, 1) // width
    out = []
    for b in range(groups):
        total = parts[b]
        for g in range(groups):
            if g != b:
                total = jnp.where(lane == g, pltpu.roll(parts[g], (g - b) * width % LANES, 1), total)
        out.append(total)
    return out


def assemble_kernel(n_grp, width, by_source, by_partner, hessian, gradient, total):
    rows, columns = hessian.shape[2], hessian.shape[3]
    grad_rows = gradient.shape[0]
    packed_rows = by_source.shape[1]
    groups = LANES // width
    scan_index, group_index = lax.axis_index("scan"), lax.axis_index("grp")
    cells = rows * columns
    total[...] = jnp.zeros_like(total)
    step = 2 * groups

    def place(ids, first, size):
        local = ids - first
        return local, (local >= 0) & (local < size)

    def add(read, sign):
        def body(i, _):
            turned = []
            for half in range(2):
                parts = [read(i * step + half * groups + g) for g in range(groups)]
                turned.append(jnp.concatenate(regroup(parts, width), axis=0))
            values = jnp.concatenate(turned, axis=1)
            source, partner = values[27:28, :].astype(jnp.int32), values[28:29, :].astype(jnp.int32)
            own, other = (source, partner) if sign > 0 else (partner, source)
            row, row_ok = place(own, scan_index * rows, rows)
            plus, plus_ok = place(own, group_index * columns, columns)
            minus, minus_ok = place(other, group_index * columns, columns)
            plus = jnp.where(row_ok & plus_ok, row * columns + plus, -1)
            minus = jnp.where(row_ok & minus_ok, row * columns + minus, -1)
            grad, grad_ok = place(row, group_index * grad_rows, grad_rows)
            grad = jnp.where(row_ok & grad_ok, grad, -1)
            cell = lax.broadcasted_iota(jnp.int32, (cells, 2 * LANES), 0)
            chosen = jnp.where(cell == plus, 1.0, jnp.where(cell == minus, -1.0, 0.0))
            short = lax.broadcasted_iota(jnp.int32, (16, 2 * LANES), 0)
            chosen_grad = jnp.where(short == grad, float(sign), 0.0)
            matrix = jnp.concatenate([chosen, chosen_grad], axis=0).astype(jnp.bfloat16)
            high = values.astype(jnp.bfloat16)
            low = (values - high.astype(jnp.float32)).astype(jnp.bfloat16)
            both = jnp.concatenate([high, low], axis=0)
            total[...] += lax.dot_general(
                matrix, both, (((1,), (1,)), ((), ())), preferred_element_type=jnp.float32
            )
            return 0

        return body

    blocks = by_source.shape[0]
    n_scan = by_partner.shape[1]
    lax.fori_loop(0, blocks // step, add(lambda k: by_source[k], 1), 0)
    lax.fori_loop(0, blocks // step, add(lambda k: by_partner[k // n_scan, k % n_scan], -1), 0)
    result = total[:, 0:VALUES] + total[:, VALUES : 2 * VALUES]
    turned = result[0:cells, :].T
    where = {pair: q for q, pair in enumerate(PAIRS)}
    for i in range(6):
        ids = [where[min(i, j), max(i, j)] for j in range(6)]
        band = jnp.concatenate([turned[q : q + 1, :] for q in ids], axis=0)
        for r in range(rows):
            hessian[i, :, r, :] = band[:, r * columns : (r + 1) * columns]
    gradient[...] = result[cells : cells + grad_rows, 21:27]


def local(samples, point_count, corr_scan, corr_tile, corr_src):
    f32, i32 = jnp.float32, jnp.int32
    scan_local = samples.shape[0]
    request_count = scan_local * corr_scan.shape[1]
    n_scan, n_grp = lax.axis_size("scan"), lax.axis_size("grp")
    devices = n_scan * n_grp
    cap = 2 * request_count // devices
    width = n_grp * cap
    packed_rows = VALUES * width // LANES
    columns = scan_local * n_scan // n_grp
    grad_rows = scan_local // n_grp
    shape = jax.ShapeDtypeStruct
    dma = pltpu.SemaphoreType.DMA

    tiles = samples.transpose(0, 2, 1, 3)
    data, meta = pl.pallas_call(
        functools.partial(pack_kernel, cap, n_grp),
        out_shape=(shape((devices * cap * 4, LANES), f32), shape((devices, 1, LANES), i32)),
        in_specs=[VMEM, SMEM, SMEM, SMEM, VMEM],
        out_specs=(VMEM, SMEM),
        scratch_shapes=[pltpu.SMEM((devices,), i32)],
    )(tiles, point_count, corr_scan, corr_tile, corr_src)

    by_source, by_partner = pl.pallas_call(
        functools.partial(exchange_kernel, cap, n_grp),
        out_shape=(
            shape((devices, packed_rows, LANES), f32),
            shape((n_grp, n_scan, packed_rows, LANES), f32),
        ),
        in_specs=[VMEM, SMEM, VMEM, VMEM],
        out_specs=(VMEM, VMEM),
        scratch_shapes=[
            pltpu.VMEM(data.shape, f32),
            pltpu.VMEM(meta.shape, i32),
            pltpu.SMEM(meta.shape, i32),
            pltpu.VMEM((9, 16, LANES), f32),
            pltpu.VMEM((LANES, LANES), f32),
            pltpu.VMEM((n_scan, packed_rows, LANES), f32),
        ]
        + [dma((devices,))] * 6
        + [dma((n_grp, n_scan))] * 2
        + [dma((3,))],
        compiler_params=pltpu.CompilerParams(collective_id=0, has_side_effects=True),
    )(tiles, point_count, data, meta)

    hessian, gradient = pl.pallas_call(
        functools.partial(assemble_kernel, n_grp, width),
        out_shape=(shape((6, 6, scan_local, columns), f32), shape((grad_rows, 6), f32)),
        in_specs=[VMEM, VMEM],
        out_specs=(VMEM, VMEM),
        scratch_shapes=[pltpu.VMEM((scan_local * columns + 16, 2 * VALUES), f32)],
    )(by_source, by_partner)
    return hessian.transpose(2, 0, 1, 3), gradient


def solution(mesh):
    placed = (
        P("scan", "grp", None, None),
        P("scan"),
        P("scan", "grp"),
        P("scan", "grp"),
        P("scan", "grp", None),
    )
    return jax.shard_map(
        local,
        mesh=mesh,
        in_specs=placed,
        out_specs=(P("scan", None, None, "grp"), P(("scan", "grp"), None)),
        check_vma=False,
    )
```

time: 83.6 us -> 64.8 us (0.78)
  Pallas kernels: 78.4 us -> 64 us
  local copies, waits for them, and re-layouts: 4.17 us -> 0 us
    pallas_call x3 -> x1, Pallas kernels: 63 us -> 49.4 us  [local(): pl.pallas_call(functools.partial(exchange_kernel, cap, n_grp), out_shape=...]
    unnamed x1 -> x0, local copies, waits for them, and re-layouts: 2.36 us -> none
    pallas_call x1 -> x0, local copies, waits for them, and re-layouts: 1.81 us -> none  [local(): pl.pallas_call(functools.partial(assemble_kernel, n_grp, width), out_shap...]
    pallas_call x1, Pallas kernels: 8.06 us -> 6.87 us  [local(): pl.pallas_call(functools.partial(pack_kernel, cap, n_grp), out_shape=(sha...]
where the time goes in v2:
time: 64.8 us; the launch traced here: 64.6 us
  Pallas kernels  64 us (99%)
  between operations  0.65 us (1%)
    pallas_call x1, Pallas kernels, local(): pl.pallas_call(functools.partial(exchange_kernel, cap, n_grp), out_shape=...  49.4 us
    pallas_call x1, Pallas kernels, local(): pl.pallas_call(functools.partial(assemble_kernel, n_grp, width), out_shap...  7.68 us
    pallas_call x1, Pallas kernels, local(): pl.pallas_call(functools.partial(pack_kernel, cap, n_grp), out_shape=(sha...  6.87 us

profile of v2, /device:TPU:0, one launch (start us, length us, event | category | flops | bytes accessed | tf_op | source)
XLA Modules:
  0.0 64.6 jit_solution(3960750469469286774)
XLA Ops:
  0.6 6.9 %shard_map.68 = (f32[2048,128]{1,0:T(8,128)}, s32[32,1,128]{2,1,0:T(1,128)}) custom-call(f32[16,6,16,128]{3,2,1,0:T(8,128)} %bitcast.2, s32[16]{0:T(128)} %count.3, s32[16,16]{1,0:T(8,128)} %corr_scan.1, s32[16,16]{1,0:T(8,128)} %corr_tile.1, s32[16,16,128]{2,1,0:T(8,128)} %corr_src.1), custom_call_target="tpu_custom_call" | custom-call | tf_op jit(solution)/shard_map/pallas_call | solution.py:340
  7.5 49.4 %shard_map.69 = (f32[32,16,128]{2,1,0:T(8,128)}, f32[4,8,16,128]{3,2,1,0:T(8,128)}) custom-call(f32[16,6,16,128]{3,2,1,0:T(8,128)} %bitcast.3, s32[16]{0:T(128)} %count.3, f32[2048,128]{1,0:T(8,128)} %get-tuple-element.8.data, s32[32,1,128]{2,1,0:T(1,128)} %get-tuple-element.9.meta), custom_call_target="tpu_custom_call" | custom-call | tf_op jit(solution)/shard_map/pallas_call | solution.py:348
  56.9 7.7 %shard_map.70 = (f32[6,6,16,32]{3,2,1,0:T(8,128)}, f32[4,6]{1,0:T(4,128)}) custom-call(f32[32,16,128]{2,1,0:T(8,128)} %get-tuple-element.10.by_source, f32[4,8,16,128]{3,2,1,0:T(8,128)} %get-tuple-element.11.by_partner), custom_call_target="tpu_custom_call" | custom-call | tf_op jit(solution)/shard_map/pallas_call | solution.py:370

commit v3 on v2

--- a/solution.py
+++ b/solution.py
@@ -9,6 +9,7 @@
 
 LANES = 128
 VALUES = 32
+LEAST_POINTS = 4096
 PAIRS = [(i, j) for i in range(6) for j in range(i, 6)]
 VMEM = pl.BlockSpec(memory_space=pltpu.VMEM)
 SMEM = pl.BlockSpec(memory_space=pltpu.SMEM)
@@ -62,9 +63,9 @@
             meta[d, 0, j] = b_loc
             meta[d, 0, cap + j] = t_loc
             meta[d, 0, 2 * cap + j] = scan_index * scan_local + s
-            base = (d * cap + j) * 4
+            base = d * cap * 4 + j
             for c in range(4):
-                data[pl.ds(base + c, 1), :] = picked[c][k : k + 1, :]
+                data[pl.ds(base + c * cap, 1), :] = picked[c][k : k + 1, :]
         return 0
 
     lax.fori_loop(0, scan_local, one_scan, 0)
@@ -92,9 +93,9 @@
 
 
 def exchange_kernel(
-    cap, n_grp, samples, count, data, meta, by_source, by_partner,
-    data_in, meta_in, codes, comps, sums, packed,
-    send_data, recv_data, send_meta, recv_meta, send_src, recv_src, send_part, recv_part, own,
+    cap, n_grp, samples, count, data, meta, hessian, gradient,
+    data_in, meta_in, codes, comps, sums, packed, by_source, by_partner, total_ref,
+    send_data, recv_data, send_meta, recv_meta, send_src, recv_src, send_next, send_part, recv_part, own,
 ):
     scan_local, tiles_local = samples.shape[0], samples.shape[2]
     n_scan, packed_rows = packed.shape[0], packed.shape[1]
@@ -108,12 +109,14 @@
     lane = lax.broadcasted_iota(jnp.int32, (batch, LANES), 1)
     packed_lane = lax.broadcasted_iota(jnp.int32, (packed_rows, LANES), 1) // width
 
-    def part(d):
-        return pl.ds(pl.multiple_of(d * rows, rows), rows)
-
-    def send_one(src, dst_index, send_index, recv_index, peer):
+    full_groups = min(LEAST_POINTS // (tiles_local * LANES), n_grp) if 3 * cap % 8 == 0 else 0
+    short = rows - cap
+
+    def send_one(src, dst_index, send_index, recv_index, peer, size):
         return remote(
-            data.at[part(src)], data_in.at[part(dst_index)], send_data.at[send_index], recv_data.at[recv_index], peer, n_grp
+            data.at[pl.ds(pl.multiple_of(src * rows, 8), size)],
+            data_in.at[pl.ds(pl.multiple_of(dst_index * rows, 8), size)],
+            send_data.at[send_index], recv_data.at[recv_index], peer, n_grp,
         )
 
     def send_code(src, dst_index, send_index, recv_index, peer):
@@ -121,8 +124,14 @@
             meta.at[src], meta_in.at[dst_index], send_meta.at[send_index], recv_meta.at[recv_index], peer, n_grp
         )
 
-    def to_source(row, holder, peer, recv_index):
-        return remote(packed.at[row], by_source.at[holder], send_src.at[peer], recv_src.at[recv_index], peer, n_grp)
+    def to_source(row, holder, peer, send_sem):
+        return remote(packed.at[row], by_source.at[holder], send_sem, recv_src.at[holder], peer, n_grp)
+
+    def hand_on(holder, g):
+        return remote(
+            by_source.at[holder], by_source.at[holder], send_next.at[g, holder // n_grp], recv_src.at[holder],
+            scan_index * n_grp + g, n_grp,
+        )
 
     def to_partner(row, at, g):
         peer = scan_index * n_grp + g
@@ -139,7 +148,15 @@
 
     def start_data(k, _):
         peer = lax.rem(me + k, devices)
-        send_one(peer, me, peer, me, peer).start()
+
+        @pl.when(group_index < full_groups)
+        def _():
+            send_one(peer, me, peer, me, peer, short).start()
+
+        @pl.when(group_index >= full_groups)
+        def _():
+            send_one(peer, me, peer, me, peer, rows).start()
+
         return 0
 
     def wait_meta(k, _):
@@ -151,13 +168,24 @@
 
     lax.fori_loop(1, devices, start_meta, 0)
     lax.fori_loop(1, devices, start_data, 0)
-    own_data = pltpu.make_async_copy(data.at[part(me)], data_in.at[part(me)], own.at[0])
+    own_data = pltpu.make_async_copy(
+        data.at[pl.ds(pl.multiple_of(me * rows, 8), rows)], data_in.at[pl.ds(pl.multiple_of(me * rows, 8), rows)], own.at[0]
+    )
     own_meta = pltpu.make_async_copy(meta.at[me], meta_in.at[me], own.at[1])
     own_data.start()
     own_meta.start()
     sums[...] = jnp.zeros_like(sums)
     own_data.wait()
     own_meta.wait()
+    total_ref[...] = jnp.zeros_like(total_ref)
+
+    def no_mask(row, _):
+        for g in range(full_groups):
+            first = pl.multiple_of((row * n_grp + g) * rows + short, 8)
+            data_in[pl.ds(first, cap), :] = jnp.ones((cap, LANES), jnp.float32)
+        return 0
+
+    lax.fori_loop(0, n_scan, no_mask, 0)
     lax.fori_loop(1, devices, wait_meta, 0)
     to_scalar = pltpu.make_async_copy(meta_in, codes, own.at[2])
     to_scalar.start()
@@ -177,8 +205,16 @@
             comps[6, j : j + 1, :] = jnp.full((1, LANES), limit.astype(jnp.float32))
             comps[7, j : j + 1, :] = jnp.full((1, LANES), partner.astype(jnp.float32))
             comps[8, j : j + 1, :] = jnp.full((1, LANES), source.astype(jnp.float32))
-        base = (row * width + i * batch) * 4
-        px, py, pz, mask = [data_in[pl.ds(base + c, batch, stride=4), :] for c in range(4)]
+        count_in = max(batch // cap, 1)
+        read = []
+        for c in range(4):
+            pieces = []
+            for piece in range(count_in):
+                step, place = halves(i * batch + piece * cap, cap)
+                base = (row * n_grp + step) * rows + c * cap + place
+                pieces.append(data_in[pl.ds(base, min(batch, cap)), :])
+            read.append(pieces[0] if count_in == 1 else jnp.concatenate(pieces, axis=0))
+        px, py, pz, mask = read
         valid = lane < comps[6].astype(jnp.int32)
         nx, ny, nz = [jnp.where(valid, comps[c], 0.0) for c in (3, 4, 5)]
         residual = nx * (px - comps[0]) + ny * (py - comps[1]) + nz * (pz - comps[2])
@@ -201,7 +237,7 @@
 
             @pl.when(source != me)
             def _():
-                send_one(source, source, source, source, source).wait_recv()
+                send_one(source, source, source, source, source, short if g < full_groups else rows).wait_recv()
 
         lax.fori_loop(0, width // batch, one_batch, row)
         turned = sums[...].T
@@ -211,42 +247,130 @@
             result = jnp.where(packed_lane == g, moved, result)
         packed[row] = result
         by_partner[group_index, row] = result
-        for g in range(n_grp):
-            peer = row * n_grp + g
-
-            @pl.when(peer != me)
-            def _():
-                to_source(row, me, peer, me).start()
-
-        @pl.when(row == scan_index)
-        def _():
-            by_source[me] = result
-
         for g in range(1, n_grp):
             to_partner(row, group_index, lax.rem(group_index + g, n_grp)).start()
-        return 0
+
+        @pl.when(row != scan_index)
+        def _():
+            to_source(row, me, row * n_grp + group_index, send_src.at[row]).start()
+
+        @pl.when(k >= lag)
+        def _():
+            add_partner(k - lag)
+
+        return 0
+
+    lag = 3
+    rows_out, columns = hessian.shape[2], hessian.shape[3]
+    grad_rows = gradient.shape[0]
+    cells = rows_out * columns
+
+    def add(blocks, sign):
+        blocks = blocks + [jnp.zeros_like(blocks[0])] * (-n_grp % groups)
+        turned = []
+        for first in range(0, len(blocks), groups):
+            turned.append(jnp.concatenate(regroup(blocks[first : first + groups], width), axis=0))
+        values = jnp.concatenate(turned, axis=1)
+        slots = values.shape[1]
+        source, partner = values[27:28, :].astype(jnp.int32), values[28:29, :].astype(jnp.int32)
+        mine, other = (source, partner) if sign > 0 else (partner, source)
+        row = mine - scan_index * rows_out
+        row_ok = (row >= 0) & (row < rows_out)
+        plus, minus = mine - group_index * columns, other - group_index * columns
+        plus = jnp.where(row_ok & (plus >= 0) & (plus < columns), row * columns + plus, -1)
+        minus = jnp.where(row_ok & (minus >= 0) & (minus < columns), row * columns + minus, -1)
+        grad = row - group_index * grad_rows
+        grad = jnp.where(row_ok & (grad >= 0) & (grad < grad_rows), grad, -1)
+        cell = lax.broadcasted_iota(jnp.int32, (cells, slots), 0)
+        chosen = jnp.where(cell == plus, 1.0, jnp.where(cell == minus, -1.0, 0.0))
+        few = lax.broadcasted_iota(jnp.int32, (16, slots), 0)
+        chosen_grad = jnp.where(few == grad, float(sign), 0.0)
+        matrix = jnp.concatenate([chosen, chosen_grad], axis=0).astype(jnp.bfloat16)
+        high = values.astype(jnp.bfloat16)
+        low = (values - high.astype(jnp.float32)).astype(jnp.bfloat16)
+        both = jnp.concatenate([high, low], axis=0)
+        total_ref[...] += lax.dot_general(
+            matrix, both, (((1,), (1,)), ((), ())), preferred_element_type=jnp.float32
+        )
+
+    def add_partner(k):
+        row = lax.rem(scan_index + n_scan - k, n_scan)
+        for g in range(1, n_grp):
+            at = lax.rem(group_index + g, n_grp)
+            to_partner(row, at, at).wait_recv()
+        add([by_partner[g, row] for g in range(n_grp)], -1)
 
     lax.fori_loop(0, n_scan, one_row, 0)
+
+    def last_partner(k, _):
+        add_partner(k)
+        return 0
+
+    lax.fori_loop(max(n_scan - lag, 0), n_scan, last_partner, 0)
+
+    def pass_on(k, _):
+        row = lax.rem(scan_index + k, n_scan)
+        holder = row * n_grp + group_index
+        to_source(row, holder, holder, send_src.at[row]).wait_recv()
+        for g in range(1, n_grp):
+            hand_on(holder, lax.rem(group_index + g, n_grp)).start()
+
+        @pl.when(k > 1)
+        def _():
+            add_source(k - 1)
+
+        return 0
+
+    def add_source(k):
+        row = lax.rem(scan_index + k, n_scan)
+        for g in range(1, n_grp):
+            holder = row * n_grp + lax.rem(group_index + g, n_grp)
+            to_source(row, holder, holder, send_src.at[row]).wait_recv()
+        add([by_source[row * n_grp + g] for g in range(n_grp)], 1)
+
+    add([by_partner[g, scan_index] for g in range(n_grp)], 1)
+    lax.fori_loop(1, n_scan, pass_on, 0)
+    add_source(n_scan - 1)
+
+    result = total_ref[:, 0:VALUES] + total_ref[:, VALUES : 2 * VALUES]
+    turned = result[0:cells, :].T
+    where = {pair: q for q, pair in enumerate(PAIRS)}
+    for i in range(6):
+        ids = [where[min(i, j), max(i, j)] for j in range(6)]
+        band = jnp.concatenate([turned[q : q + 1, :] for q in ids], axis=0)
+        for r in range(rows_out):
+            hessian[i, :, r, :] = band[:, r * columns : (r + 1) * columns]
+    gradient[...] = result[cells : cells + grad_rows, 21:27]
 
     def finish(k, _):
         peer = lax.rem(me + k, devices)
-        send_one(peer, peer, peer, peer, peer).wait_send()
-        copy = to_source(0, peer, peer, peer)
-        copy.wait_send()
-        copy.wait_recv()
+
+        @pl.when(group_index < full_groups)
+        def _():
+            send_one(peer, peer, peer, peer, peer, short).wait_send()
+
+        @pl.when(group_index >= full_groups)
+        def _():
+            send_one(peer, peer, peer, peer, peer, rows).wait_send()
+
         return 0
 
     lax.fori_loop(1, devices, finish, 0)
 
-    def finish_partner(row, _):
-        for k in range(1, n_grp):
-            g = lax.rem(group_index + k, n_grp)
-            copy = to_partner(row, g, g)
-            copy.wait_send()
-            copy.wait_recv()
-        return 0
-
-    lax.fori_loop(0, n_scan, finish_partner, 0)
+    def finish_rows(k, _):
+        row = lax.rem(scan_index + k, n_scan)
+        for j in range(1, n_grp):
+            to_partner(row, group_index, lax.rem(group_index + j, n_grp)).wait_send()
+
+        @pl.when(k > 0)
+        def _():
+            to_source(row, me, row * n_grp + group_index, send_src.at[row]).wait_send()
+            for j in range(1, n_grp):
+                hand_on(row * n_grp + group_index, lax.rem(group_index + j, n_grp)).wait_send()
+
+        return 0
+
+    lax.fori_loop(0, n_scan, finish_rows, 0)
 
 
 def regroup(parts, width):
@@ -260,66 +384,6 @@
                 total = jnp.where(lane == g, pltpu.roll(parts[g], (g - b) * width % LANES, 1), total)
         out.append(total)
     return out
-
-
-def assemble_kernel(n_grp, width, by_source, by_partner, hessian, gradient, total):
-    rows, columns = hessian.shape[2], hessian.shape[3]
-    grad_rows = gradient.shape[0]
-    packed_rows = by_source.shape[1]
-    groups = LANES // width
-    scan_index, group_index = lax.axis_index("scan"), lax.axis_index("grp")
-    cells = rows * columns
-    total[...] = jnp.zeros_like(total)
-    step = 2 * groups
-
-    def place(ids, first, size):
-        local = ids - first
-        return local, (local >= 0) & (local < size)
-
-    def add(read, sign):
-        def body(i, _):
-            turned = []
-            for half in range(2):
-                parts = [read(i * step + half * groups + g) for g in range(groups)]
-                turned.append(jnp.concatenate(regroup(parts, width), axis=0))
-            values = jnp.concatenate(turned, axis=1)
-            source, partner = values[27:28, :].astype(jnp.int32), values[28:29, :].astype(jnp.int32)
-            own, other = (source, partner) if sign > 0 else (partner, source)
-            row, row_ok = place(own, scan_index * rows, rows)
-            plus, plus_ok = place(own, group_index * columns, columns)
-            minus, minus_ok = place(other, group_index * columns, columns)
-            plus = jnp.where(row_ok & plus_ok, row * columns + plus, -1)
-            minus = jnp.where(row_ok & minus_ok, row * columns + minus, -1)
-            grad, grad_ok = place(row, group_index * grad_rows, grad_rows)
-            grad = jnp.where(row_ok & grad_ok, grad, -1)
-            cell = lax.broadcasted_iota(jnp.int32, (cells, 2 * LANES), 0)
-            chosen = jnp.where(cell == plus, 1.0, jnp.where(cell == minus, -1.0, 0.0))
-            short = lax.broadcasted_iota(jnp.int32, (16, 2 * LANES), 0)
-            chosen_grad = jnp.where(short == grad, float(sign), 0.0)
-            matrix = jnp.concatenate([chosen, chosen_grad], axis=0).astype(jnp.bfloat16)
-            high = values.astype(jnp.bfloat16)
-            low = (values - high.astype(jnp.float32)).astype(jnp.bfloat16)
-            both = jnp.concatenate([high, low], axis=0)
-            total[...] += lax.dot_general(
-                matrix, both, (((1,), (1,)), ((), ())), preferred_element_type=jnp.float32
-            )
-            return 0
-
-        return body
-
-    blocks = by_source.shape[0]
-    n_scan = by_partner.shape[1]
-    lax.fori_loop(0, blocks // step, add(lambda k: by_source[k], 1), 0)
-    lax.fori_loop(0, blocks // step, add(lambda k: by_partner[k // n_scan, k % n_scan], -1), 0)
-    result = total[:, 0:VALUES] + total[:, VALUES : 2 * VALUES]
-    turned = result[0:cells, :].T
-    where = {pair: q for q, pair in enumerate(PAIRS)}
-    for i in range(6):
-        ids = [where[min(i, j), max(i, j)] for j in range(6)]
-        band = jnp.concatenate([turned[q : q + 1, :] for q in ids], axis=0)
-        for r in range(rows):
-            hessian[i, :, r, :] = band[:, r * columns : (r + 1) * columns]
-    gradient[...] = result[cells : cells + grad_rows, 21:27]
 
 
 def local(samples, point_count, corr_scan, corr_tile, corr_src):
@@ -345,12 +409,9 @@
         scratch_shapes=[pltpu.SMEM((devices,), i32)],
     )(tiles, point_count, corr_scan, corr_tile, corr_src)
 
-    by_source, by_partner = pl.pallas_call(
+    hessian, gradient = pl.pallas_call(
         functools.partial(exchange_kernel, cap, n_grp),
-        out_shape=(
-            shape((devices, packed_rows, LANES), f32),
-            shape((n_grp, n_scan, packed_rows, LANES), f32),
-        ),
+        out_shape=(shape((6, 6, scan_local, columns), f32), shape((grad_rows, 6), f32)),
         in_specs=[VMEM, SMEM, VMEM, VMEM],
         out_specs=(VMEM, VMEM),
         scratch_shapes=[
@@ -360,20 +421,16 @@
             pltpu.VMEM((9, 16, LANES), f32),
             pltpu.VMEM((LANES, LANES), f32),
             pltpu.VMEM((n_scan, packed_rows, LANES), f32),
+            pltpu.VMEM((devices, packed_rows, LANES), f32),
+            pltpu.VMEM((n_grp, n_scan, packed_rows, LANES), f32),
+            pltpu.VMEM((scan_local * columns + 16, 2 * VALUES), f32),
         ]
-        + [dma((devices,))] * 6
-        + [dma((n_grp, n_scan))] * 2
+        + [dma((devices,))] * 4
+        + [dma((n_scan,)), dma((devices,))]
+        + [dma((n_grp, n_scan))] * 3
         + [dma((3,))],
         compiler_params=pltpu.CompilerParams(collective_id=0, has_side_effects=True),
     )(tiles, point_count, data, meta)
-
-    hessian, gradient = pl.pallas_call(
-        functools.partial(assemble_kernel, n_grp, width),
-        out_shape=(shape((6, 6, scan_local, columns), f32), shape((grad_rows, 6), f32)),
-        in_specs=[VMEM, VMEM],
-        out_specs=(VMEM, VMEM),
-        scratch_shapes=[pltpu.VMEM((scan_local * columns + 16, 2 * VALUES), f32)],
-    )(by_source, by_partner)
     return hessian.transpose(2, 0, 1, 3), gradient
 
 

time: 64.8 us -> 65.4 us (level)
  the two profiles are of different devices: /device:TPU:0 before, /device:TPU:29 now
where the time goes in v3:
time: 65.4 us; the launch traced here: 65.2 us
  Pallas kernels  62.2 us (95%)
  local copies, waits for them, and re-layouts  2.28 us (3%)
  between operations  0.66 us (1%)
    pallas_call x1, Pallas kernels, local(): pl.pallas_call(functools.partial(exchange_kernel, cap, n_grp), out_shape=...  55.5 us
    pallas_call x1, Pallas kernels, local(): pl.pallas_call(functools.partial(pack_kernel, cap, n_grp), out_shape=(sha...  6.73 us
    unnamed x4, local copies, waits for them, and re-layouts  2.28 us

profile of v3, /device:TPU:29, one launch (start us, length us, event | category | flops | bytes accessed | tf_op | source)
XLA Modules:
  0.0 65.2 jit_solution(10904485660366691060)
XLA Ops:
  0.6 6.7 %shard_map.68 = (f32[2048,128]{1,0:T(8,128)}, s32[32,1,128]{2,1,0:T(1,128)}) custom-call(f32[16,6,16,128]{3,2,1,0:T(8,128)} %bitcast.2, s32[16]{0:T(128)} %count.3, s32[16,16]{1,0:T(8,128)} %corr_scan.1, s32[16,16]{1,0:T(8,128)} %corr_tile.1, s32[16,16,128]{2,1,0:T(8,128)} %corr_src.1), custom_call_target="tpu_custom_call" | custom-call | tf_op jit(solution)/shard_map/pallas_call | solution.py:404
  7.4 55.5 %shard_map.69 = (f32[6,6,16,32]{3,2,1,0:T(8,128)}, f32[4,6]{1,0:T(4,128)}) custom-call(f32[16,6,16,128]{3,2,1,0:T(8,128)} %bitcast.3, s32[16]{0:T(128)} %count.3, f32[2048,128]{1,0:T(8,128)} %get-tuple-element.6.data, s32[32,1,128]{2,1,0:T(1,128)} %get-tuple-element.7.meta), custom_call_target="tpu_custom_call" | custom-call | tf_op jit(solution)/shard_map/pallas_call | solution.py:412
  62.9 0.0 copy-start
  62.9 1.7 %copy.9 = f32[16,6,6,32]{3,0,2,1:T(8,128)} copy(f32[16,6,6,32]{3,0,2,1:T(8,128)} %bitcast.4) | data formatting | bytes 147456
  64.6 0.0 copy-done
  64.6 0.6 copy.10
Async XLA Ops:
  62.9 1.7 %copy-start = (f32[4,6]{1,0:T(4,128)S(1)}, f32[4,6]{1,0:T(4,128)}, u32[]{:S(2)}) copy-start(f32[4,6]{1,0:T(4,128)} %get-tuple-element.13) | copy-start | bytes 292

commit v4 on v2

--- a/solution.py
+++ b/solution.py
@@ -9,6 +9,7 @@
 
 LANES = 128
 VALUES = 32
+LEAST_POINTS = 4096
 PAIRS = [(i, j) for i in range(6) for j in range(i, 6)]
 VMEM = pl.BlockSpec(memory_space=pltpu.VMEM)
 SMEM = pl.BlockSpec(memory_space=pltpu.SMEM)
@@ -62,9 +63,9 @@
             meta[d, 0, j] = b_loc
             meta[d, 0, cap + j] = t_loc
             meta[d, 0, 2 * cap + j] = scan_index * scan_local + s
-            base = (d * cap + j) * 4
+            base = d * cap * 4 + j
             for c in range(4):
-                data[pl.ds(base + c, 1), :] = picked[c][k : k + 1, :]
+                data[pl.ds(base + c * cap, 1), :] = picked[c][k : k + 1, :]
         return 0
 
     lax.fori_loop(0, scan_local, one_scan, 0)
@@ -108,12 +109,14 @@
     lane = lax.broadcasted_iota(jnp.int32, (batch, LANES), 1)
     packed_lane = lax.broadcasted_iota(jnp.int32, (packed_rows, LANES), 1) // width
 
-    def part(d):
-        return pl.ds(pl.multiple_of(d * rows, rows), rows)
-
-    def send_one(src, dst_index, send_index, recv_index, peer):
+    full_groups = min(LEAST_POINTS // (tiles_local * LANES), n_grp) if 3 * cap % 8 == 0 else 0
+    short = rows - cap
+
+    def send_one(src, dst_index, send_index, recv_index, peer, size):
         return remote(
-            data.at[part(src)], data_in.at[part(dst_index)], send_data.at[send_index], recv_data.at[recv_index], peer, n_grp
+            data.at[pl.ds(pl.multiple_of(src * rows, 8), size)],
+            data_in.at[pl.ds(pl.multiple_of(dst_index * rows, 8), size)],
+            send_data.at[send_index], recv_data.at[recv_index], peer, n_grp,
         )
 
     def send_code(src, dst_index, send_index, recv_index, peer):
@@ -139,7 +142,15 @@
 
     def start_data(k, _):
         peer = lax.rem(me + k, devices)
-        send_one(peer, me, peer, me, peer).start()
+
+        @pl.when(group_index < full_groups)
+        def _():
+            send_one(peer, me, peer, me, peer, short).start()
+
+        @pl.when(group_index >= full_groups)
+        def _():
+            send_one(peer, me, peer, me, peer, rows).start()
+
         return 0
 
     def wait_meta(k, _):
@@ -151,13 +162,23 @@
 
     lax.fori_loop(1, devices, start_meta, 0)
     lax.fori_loop(1, devices, start_data, 0)
-    own_data = pltpu.make_async_copy(data.at[part(me)], data_in.at[part(me)], own.at[0])
+    own_data = pltpu.make_async_copy(
+        data.at[pl.ds(pl.multiple_of(me * rows, 8), rows)], data_in.at[pl.ds(pl.multiple_of(me * rows, 8), rows)], own.at[0]
+    )
     own_meta = pltpu.make_async_copy(meta.at[me], meta_in.at[me], own.at[1])
     own_data.start()
     own_meta.start()
     sums[...] = jnp.zeros_like(sums)
     own_data.wait()
     own_meta.wait()
+
+    def no_mask(row, _):
+        for g in range(full_groups):
+            first = pl.multiple_of((row * n_grp + g) * rows + short, 8)
+            data_in[pl.ds(first, cap), :] = jnp.ones((cap, LANES), jnp.float32)
+        return 0
+
+    lax.fori_loop(0, n_scan, no_mask, 0)
     lax.fori_loop(1, devices, wait_meta, 0)
     to_scalar = pltpu.make_async_copy(meta_in, codes, own.at[2])
     to_scalar.start()
@@ -177,8 +198,16 @@
             comps[6, j : j + 1, :] = jnp.full((1, LANES), limit.astype(jnp.float32))
             comps[7, j : j + 1, :] = jnp.full((1, LANES), partner.astype(jnp.float32))
             comps[8, j : j + 1, :] = jnp.full((1, LANES), source.astype(jnp.float32))
-        base = (row * width + i * batch) * 4
-        px, py, pz, mask = [data_in[pl.ds(base + c, batch, stride=4), :] for c in range(4)]
+        count_in = max(batch // cap, 1)
+        read = []
+        for c in range(4):
+            pieces = []
+            for piece in range(count_in):
+                step, place = halves(i * batch + piece * cap, cap)
+                base = (row * n_grp + step) * rows + c * cap + place
+                pieces.append(data_in[pl.ds(base, min(batch, cap)), :])
+            read.append(pieces[0] if count_in == 1 else jnp.concatenate(pieces, axis=0))
+        px, py, pz, mask = read
         valid = lane < comps[6].astype(jnp.int32)
         nx, ny, nz = [jnp.where(valid, comps[c], 0.0) for c in (3, 4, 5)]
         residual = nx * (px - comps[0]) + ny * (py - comps[1]) + nz * (pz - comps[2])
@@ -201,7 +230,7 @@
 
             @pl.when(source != me)
             def _():
-                send_one(source, source, source, source, source).wait_recv()
+                send_one(source, source, source, source, source, short if g < full_groups else rows).wait_recv()
 
         lax.fori_loop(0, width // batch, one_batch, row)
         turned = sums[...].T
@@ -230,7 +259,15 @@
 
     def finish(k, _):
         peer = lax.rem(me + k, devices)
-        send_one(peer, peer, peer, peer, peer).wait_send()
+
+        @pl.when(group_index < full_groups)
+        def _():
+            send_one(peer, peer, peer, peer, peer, short).wait_send()
+
+        @pl.when(group_index >= full_groups)
+        def _():
+            send_one(peer, peer, peer, peer, peer, rows).wait_send()
+
         copy = to_source(0, peer, peer, peer)
         copy.wait_send()
         copy.wait_recv()

time: 64.8 us -> 63.8 us (0.985)
  Pallas kernels: 64 us -> 63 us
    pallas_call x1, Pallas kernels: 49.4 us -> 48.6 us  [local(): pl.pallas_call(functools.partial(exchange_kernel, cap, n_grp), out_shape=...]
where the time goes in v4:
time: 63.8 us; the launch traced here: 63.7 us
  Pallas kernels  63 us (99%)
  between operations  0.65 us (1%)
    pallas_call x1, Pallas kernels, local(): pl.pallas_call(functools.partial(exchange_kernel, cap, n_grp), out_shape=...  48.6 us
    pallas_call x1, Pallas kernels, local(): pl.pallas_call(functools.partial(assemble_kernel, n_grp, width), out_shap...  7.69 us
    pallas_call x1, Pallas kernels, local(): pl.pallas_call(functools.partial(pack_kernel, cap, n_grp), out_shape=(sha...  6.73 us

profile of v4, /device:TPU:0, one launch (start us, length us, event | category | flops | bytes accessed | tf_op | source)
XLA Modules:
  0.0 63.7 jit_solution(13091038301344580034)
XLA Ops:
  0.6 6.7 %shard_map.68 = (f32[2048,128]{1,0:T(8,128)}, s32[32,1,128]{2,1,0:T(1,128)}) custom-call(f32[16,6,16,128]{3,2,1,0:T(8,128)} %bitcast.2, s32[16]{0:T(128)} %count.3, s32[16,16]{1,0:T(8,128)} %corr_scan.1, s32[16,16]{1,0:T(8,128)} %corr_tile.1, s32[16,16,128]{2,1,0:T(8,128)} %corr_src.1), custom_call_target="tpu_custom_call" | custom-call | tf_op jit(solution)/shard_map/pallas_call | solution.py:377
  7.4 48.6 %shard_map.69 = (f32[32,16,128]{2,1,0:T(8,128)}, f32[4,8,16,128]{3,2,1,0:T(8,128)}) custom-call(f32[16,6,16,128]{3,2,1,0:T(8,128)} %bitcast.3, s32[16]{0:T(128)} %count.3, f32[2048,128]{1,0:T(8,128)} %get-tuple-element.8.data, s32[32,1,128]{2,1,0:T(1,128)} %get-tuple-element.9.meta), custom_call_target="tpu_custom_call" | custom-call | tf_op jit(solution)/shard_map/pallas_call | solution.py:385
  56.0 7.7 %shard_map.70 = (f32[6,6,16,32]{3,2,1,0:T(8,128)}, f32[4,6]{1,0:T(4,128)}) custom-call(f32[32,16,128]{2,1,0:T(8,128)} %get-tuple-element.10.by_source, f32[4,8,16,128]{3,2,1,0:T(8,128)} %get-tuple-element.11.by_partner), custom_call_target="tpu_custom_call" | custom-call | tf_op jit(solution)/shard_map/pallas_call | solution.py:407
